TPU v7x, 32 devices: a whole 2x2x4 slice. The times are simulated.
32 devices in a mesh: gx: 2 (over x), gy: 4 (over z), gz: 4 (over y, core).
Axes of the slice: x: 2, y: 2, z: 4, core: 2. Of those that a mesh axis runs over, the one named last changes fastest.
Arguments:
- fields: float32 [1, 64, 128, 512], P(None, 'gx', 'gy', 'gz'), may hold values from -13 to 13
- exponents: int32 [5], replicated, may hold values from -5 to -1
Outputs:
- coefficients: float32 [1, 64, 128, 512], P(None, 'gx', 'gy', 'gz')
- statistics: float32 [2, 1, 5], replicated
All inputs are finite; a program needn't handle non-finite values.
Results may differ from a plain program's by a relative error of at most 0.0003.
Values sent between devices are 32-bit elements; how exact they have to be, the bound alone decides.
A program may use at most 64 MiB of HBM per device.

v0:
```python
import functools

import numpy as np

import jax
import jax.numpy as jnp
from jax import lax
from jax.experimental import pallas as pl
from jax.experimental.pallas import tpu as pltpu
from jax.sharding import PartitionSpec as P

FINE = 3
LEVELS = 5
LANES = 128
BUFFERS = 19
VMEM_LIMIT = 67_043_328
MESH = pl.DeviceIdType.MESH


def periodic_lift(length):
    eye = np.eye(length)
    even, odd = eye[0::2], eye[1::2]
    detail = odd - 0.5 * (even + np.roll(even, -1, 0))
    smooth = even + 0.25 * (np.roll(detail, 1, 0) + detail)
    whole = np.zeros((length, length))
    whole[0::2] = smooth
    whole[1::2] = detail
    return whole


def second_lift(length):
    whole = np.zeros((length, length))
    whole[0::2, 0::2] = periodic_lift(length // 2)
    return whole


def coarse_matrices(sizes, coarse):
    nx, ny, nz = sizes
    cx, cy, cz = coarse
    rows = np.arange(nx * ny * cx * cy)
    dev, inner = rows // (cx * cy), rows % (cx * cy)
    gx = (dev // ny) * cx + inner // cy
    gy = (dev % ny) * cy + inner % cy
    step = LANES // cz
    lanes = np.array([z * step + d for d in range(nz) for z in range(cz)])
    result = []
    for both_levels in (False, True):
        mx, my, mz = periodic_lift(nx * cx), periodic_lift(ny * cy), periodic_lift(nz * cz)
        if both_levels:
            mx, my, mz = second_lift(nx * cx) @ mx, second_lift(ny * cy) @ my, second_lift(nz * cz) @ mz
        both = mx[gx[:, None], gx[None]] * my[gy[:, None], gy[None]]
        along = np.zeros((LANES, LANES))
        along[np.ix_(lanes, lanes)] = mz.T
        result.append((both.astype(np.float32), along.astype(np.float32)))
    return [np.stack(pair) for pair in zip(*result)]


def iota(shape, axis):
    return lax.broadcasted_iota(jnp.int32, shape, axis)


def roll(values, shift, axis):
    return pltpu.roll(values, shift % values.shape[axis], axis)


def lift_rows(v, low, high):
    n = v.shape[0]
    row = iota(v.shape, 0)
    odd = row % 2 == 1
    up = jnp.where(row == n - 1, high, roll(v, -1, 0))
    w = jnp.where(odd, v - 0.5 * (roll(v, 1, 0) + up), v)
    down = jnp.where(row == 0, low - 0.5 * v, roll(w, 1, 0))
    return jnp.where(odd, w, w + 0.25 * (down + roll(w, -1, 0)))


def lift_lanes(v, rim, s):
    lane = iota(v.shape, 1)
    up = jnp.where(lane == LANES - s, rim, roll(v, -s, 1))
    w = jnp.where(lane % (2 * s) == s, v - 0.5 * (roll(v, s, 1) + up), v)
    down = jnp.where(lane == 0, rim - 0.5 * v, roll(w, s, 1))
    return jnp.where(lane % (2 * s) == 0, w + 0.25 * (down + roll(w, -s, 1)), w)


def shrink(v, thresh):
    return v - jnp.clip(v, -thresh, thresh)


def kernel(sizes, cells, exps_in, field_in, rows_in, lanes_in, out, stats, *scratch):
    nx, ny, nz = sizes
    ndev = nx * ny * nz
    scratch = list(scratch)
    field, exps, k_s, l_s, in_sem = scratch[-5:]
    scratch = scratch[:-5]
    loads = [
        pltpu.make_async_copy(a, b, in_sem.at[i])
        for i, (a, b) in enumerate(((field_in, field), (exps_in, exps), (rows_in, k_s), (lanes_in, l_s)))
    ]
    for load in loads:
        load.start()
    me = (lax.axis_index("gx"), lax.axis_index("gy"), lax.axis_index("gz"))

    def device(dx, dy, dz):
        return (
            lax.rem(me[0] + (dx + nx), nx),
            lax.rem(me[1] + (dy + ny), ny),
            lax.rem(me[2] + (dz + nz), nz),
        )

    def thresh(level):
        return jnp.exp2(jnp.full((1, LANES), exps[level].astype(jnp.float32)))

    def split(j):
        return j // (ny * nz), (j // nz) % ny, j % nz

    barrier = pltpu.get_barrier_semaphore()

    near = max(sizes) // 2 <= FINE
    greeted = {
        tuple((d + size - 1) % size if near else d for d, size in zip(spot, sizes))
        for spot in np.ndindex(*(3, 3, 3) if near else sizes)
    } - {(0, 0, 0)}
    for spot in sorted(greeted):
        pl.semaphore_signal(barrier, inc=1, device_id=device(*spot), device_id_type=MESH)
    gath, msg, rows_s, final_s, g_send, g_recv = scratch[-6:]
    sums = []
    loads[0].wait()
    loads[1].wait()
    away = (-1, 1)
    alone = nx == 2

    for level in range(FINE):
        (xs, xr, ys, yr, es, er, yl, zs, zr, hs, hr, ds, dr, cs, cr, work, nxt, send_sem, recv_sem) = scratch[
            level * BUFFERS : level * BUFFERS + BUFFERS
        ]
        s = 2**level
        n = field.shape[2] // s
        px = field.shape[1] // s
        src = field.at[0] if level == 0 else scratch[(level - 1) * BUFFERS + 16]
        lane = iota((n, LANES), 1)

        def edge(v):
            return v[0:1], v[n - 1 : n] - 0.5 * v[n - 2 : n - 1]

        e_plane = src[0]
        p_plane = src[px - 1] - 0.5 * src[px - 2]
        xs[0] = e_plane
        xs[1] = p_plane
        ys[0] = src[:, 0, :]
        ys[1] = src[:, n - 1, :] - 0.5 * src[:, n - 2, :]
        for a, plane in ((0, e_plane), (1, p_plane)):
            es[2 * a], es[2 * a + 1] = edge(plane)

        packed = jnp.zeros((n, LANES), jnp.float32)
        for x in range(px):
            v = src[x]
            u = jnp.where(lane == LANES - s, v - 0.5 * roll(v, s, 1), v)
            at = 2 * s * x
            packed = jnp.where((lane == at) | (lane == at + s), roll(u, at + s, 1), packed)
        half = 2 * s * px
        combined = packed - 0.5 * roll(packed, 2 * s, 1)
        sides = roll(jnp.where(lane < half // 2, packed, combined), half, 1)
        zs[...] = packed
        hs[...] = sides
        ds[0], ds[1] = edge(packed)
        cs[0], cs[1] = edge(sides)

        if level == 0:
            pl.semaphore_wait(barrier, len(greeted))
        copies = []
        ways = (0,) if alone else (0, 1)
        for i in (0, 1):
            for b in (0, 1):
                for a in ways:
                    copies.append((cs.at[b], cr.at[4 * a + 2 * b + i], (away[a], away[b], away[i])))
                copies.append((ds.at[b], dr.at[2 * b + i], (0, away[b], away[i])))
        for a in (0, 1):
            for b in (0, 1):
                copies.append((es.at[2 * a + b], er.at[2 * a + b], (away[a], away[b], 0)))
        for b in (0, 1):
            copies.append((ys.at[b], yr.at[b], (0, away[b], 0)))
        for i in (0, 1):
            for a in ways:
                copies.append((hs, hr.at[2 * a + i], (away[a], 0, away[i])))
        for a in (0, 1):
            copies.append((xs.at[a], xr.at[a], (away[a], 0, 0)))
        for i in (0, 1):
            copies.append((zs, zr.at[i], (0, 0, away[i])))
        flights = [
            pltpu.make_async_remote_copy(
                src_ref=f, dst_ref=t, send_sem=send_sem.at[i], recv_sem=recv_sem.at[i],
                device_id=device(*d), device_id_type=MESH,
            )
            for i, (f, t, d) in enumerate(copies)
        ]
        for flight in flights:
            flight.start()
        if level > 0:
            sums += finish()
        for flight in flights:
            flight.wait()

        for b in (0, 1):
            yl[b] = lift_rows(yr[b], er[2 + b], er[b])

        def rim_of(main, side):
            spot = iota(main(0).shape, 1)
            parts = []
            for i in (0, 1):
                after = side(0, i)
                before = after if alone else side(1, i)
                v = jnp.where(spot < half, main(i), 0.0)
                v = jnp.where((spot >= half) & (spot < half + 2 * s), after, v)
                parts.append(jnp.where(spot >= LANES - 2 * s, before, v))
            v = jnp.where(spot % (2 * s) < s, roll(parts[0], -s, 1), roll(parts[1], s, 1))
            odd = (spot // (2 * s)) % 2 == 1
            w = jnp.where(odd, v - 0.5 * (roll(v, 2 * s, 1) + roll(v, -2 * s, 1)), v)
            return jnp.where(odd, w, w + 0.25 * (roll(w, 2 * s, 1) + roll(w, -2 * s, 1)))

        rim_rows = [
            rim_of(lambda i: dr[2 * b + i], lambda a, i: cr[4 * a + 2 * b + i]) for b in (0, 1)
        ]
        rim = rim_of(lambda i: zr[i], lambda a, i: hr[2 * a + i])
        rim = lift_rows(rim, rim_rows[1], rim_rows[0])
        level_thresh = thresh(level)
        inner = (lane % (2 * s) == 0) & (iota((n, LANES), 0) % 2 == 0)
        active = lane % s == 0

        def plane_step(x, v):
            v = lift_rows(v, yl[1, x : x + 1, :], yl[0, x : x + 1, :])
            v = lift_lanes(v, roll(rim, LANES - s - 2 * s * x, 1), s)
            work[x] = v
            if x % 2 == 0:
                nxt[x // 2] = work[x, pl.ds(0, n // 2, stride=2), :]

        def finish(level=level, work=work, px=px, n=n, s=s, inner=inner, active=active, t=level_thresh):
            energy = kept = jnp.zeros((n, LANES), jnp.float32)
            for x in range(px):
                v = work[x]
                small = shrink(v, t)
                use = active & ~inner if x % 2 == 0 else active
                energy += jnp.where(use, v * v, 0.0)
                kept += jnp.where(use, jnp.abs(small), 0.0)
                if level == 0:
                    out[0, x] = small
                else:
                    spot = (0, s * x, pl.ds(0, n, stride=s), slice(None))
                    out[spot] = jnp.where(active, small, out[spot])
            return [
                jnp.sum(jnp.sum(v, axis=0, keepdims=True), axis=1, keepdims=True) for v in (energy, kept)
            ]

        even = src[0]
        before = xr[1] - 0.5 * even
        for k in range(px // 2):
            after = src[2 * k + 2] if 2 * k + 2 < px else xr[0]
            detail = src[2 * k + 1] - 0.5 * (even + after)
            smooth = even + 0.25 * (before + detail)
            plane_step(2 * k, smooth)
            plane_step(2 * k + 1, detail)
            even, before = after, detail

    last = scratch[(FINE - 1) * BUFFERS + 16]
    cx, cy = last.shape[0], last.shape[1]
    step = 2**FINE
    count = cx * cy
    for x in range(cx):
        rows_s[pl.ds(x * cy, cy), :] = last[x]
    here = rows_s[...]
    lane = iota((count, LANES), 1)
    row = iota((count, LANES), 0)
    here = jnp.where(lane % step == 0, here, 0.0)
    for bit in (1, 2, 4):
        here = jnp.where((row & bit) != 0, roll(here, bit, 1), here)
    groups = count // 8
    one = iota((1, LANES), 1)
    for g in range(groups):
        msg[g : g + 1] = jnp.sum(here[8 * g : 8 * g + 8], axis=0, keepdims=True)
    tail = jnp.zeros((1, LANES), jnp.float32)
    for i, whole in enumerate(sums + finish()):
        tail = jnp.where(one == i, whole, tail)
    msg[groups:] = jnp.broadcast_to(tail, (msg.shape[0] - groups, LANES))
    flat = (me[0] * ny + me[1]) * nz + me[2]

    def post(j):
        return pltpu.make_async_remote_copy(
            src_ref=msg, dst_ref=gath.at[flat], send_sem=g_send.at[j], recv_sem=g_recv.at[j],
            device_id=device(*split(j)), device_id_type=MESH,
        )

    def send(j, carry):
        post(ndev - j).start()
        return carry

    def settle(j, carry):
        post(j).wait()
        return carry

    if ndev <= 32:
        posts = [post(ndev - j) for j in range(1, ndev)]
        for flight in posts:
            flight.start()
        gath[flat] = msg[...]
        for flight in posts:
            flight.wait()
    else:
        lax.fori_loop(1, ndev, send, 0)
        gath[flat] = msg[...]
        lax.fori_loop(1, ndev, settle, 0)

    sub = iota((8, LANES), 0)
    lane8 = iota((8, LANES), 1)

    def unpack(d, tail):
        for g in range(groups):
            acc = jnp.zeros((8, LANES), jnp.float32)
            for z in range(nz):
                v = jnp.broadcast_to(gath[d * nz + z, g : g + 1, :], (8, LANES))
                for bit in (1, 2, 4):
                    v = jnp.where((sub & bit) != 0, roll(v, -bit, 1), v)
                acc += roll(jnp.where(lane8 % step == 0, v, 0.0), z, 1)
            final_s[pl.ds(pl.multiple_of(d * count + 8 * g, 8), 8), :] = acc
        for z in range(nz):
            tail += gath[d * nz + z, groups : groups + 1, :]
        return tail

    tail = lax.fori_loop(0, nx * ny, unpack, jnp.zeros((1, LANES), jnp.float32), unroll=nx * ny <= 8)

    def dot(a, b):
        return jnp.dot(a, b, precision=lax.Precision.HIGHEST, preferred_element_type=jnp.float32)

    grid = final_s[...]
    loads[2].wait()
    loads[3].wait()
    half3, half4 = dot(k_s[0], grid), dot(k_s[1], grid)
    grid, grid4 = dot(half3, l_s[0]), dot(half4, l_s[1])
    row = iota(grid.shape, 0)
    lane = iota(grid.shape, 1)
    inner_row = row % count
    gx, gy, gz = inner_row // cy, inner_row % cy, lane // step
    valid = lane % step < nz
    even3 = (gx % 2 == 0) & (gy % 2 == 0) & (gz % 2 == 0)
    even4 = (gx % 4 == 0) & (gy % 4 == 0) & (gz % 4 == 0)
    det3 = valid & ~even3
    det4 = valid & even3 & ~even4
    small3 = shrink(grid, thresh(FINE))
    small4 = shrink(grid4, thresh(FINE + 1))
    final_s[...] = jnp.where(even3, jnp.where(even4, grid4, small4), small3)

    def total(mask, v):
        return jnp.sum(jnp.sum(jnp.where(mask, v, 0.0), axis=0, keepdims=True), axis=1, keepdims=True)

    coarse = ((total(det3, grid * grid), total(det3, jnp.abs(small3))),
              (total(det4, grid4 * grid4), total(det4, jnp.abs(small4))))
    for q in (0, 1):
        line = jnp.zeros((1, LANES), jnp.float32)
        for level in range(LEVELS):
            weight = 8.0 ** (level + 1) / (7.0 * cells)
            if level < FINE:
                value = jnp.sum(jnp.where(one == 2 * level + q, tail, 0.0), axis=1, keepdims=True)
            else:
                value = coarse[level - FINE][q]
            line = jnp.where(one == level, value * weight, line)
        stats[q] = line[:, 0:LEVELS]

    first = pl.multiple_of((me[0] * ny + me[1]) * count, count)
    mine = pltpu.roll(final_s[pl.ds(first, count), :], lax.rem(LANES - me[2], LANES), 1)
    rows_s[...] = mine
    keep = iota((cy, LANES), 1) % step == 0
    for x in range(cx):
        spot = (0, step * x, pl.ds(0, cy, stride=step), slice(None))
        out[spot] = jnp.where(keep, rows_s[pl.ds(x * cy, cy), :], out[spot])


def shards(sizes, fields, exponents):
    nx, ny, nz = sizes
    ndev = nx * ny * nz
    _, lx, ly, lz = fields.shape
    cells = fields.size * ndev
    step = 2**FINE
    coarse = (lx // step, ly // step, lz // step)
    count = coarse[0] * coarse[1]
    tables = coarse_matrices(sizes, coarse)
    scratch = []
    for level in range(FINE):
        x, y = lx >> level, ly >> level
        scratch += [
            *(pltpu.VMEM(shape, jnp.float32) for shape in (
                (2, y, LANES), (2, y, LANES), (2, x, LANES), (2, x, LANES), (4, 1, LANES), (4, 1, LANES),
                (2, x, LANES), (y, LANES), (2, y, LANES), (y, LANES), (4, y, LANES), (2, 1, LANES),
                (4, 1, LANES), (2, 1, LANES), (8, 1, LANES), (x, y, LANES), (x // 2, y // 2, LANES),
            )),
            pltpu.SemaphoreType.DMA((26,)),
            pltpu.SemaphoreType.DMA((26,)),
        ]
    height = -(-(count // 8 + 1) // 4) * 4
    scratch += [
        pltpu.VMEM((ndev, height, LANES), jnp.float32),
        pltpu.VMEM((height, LANES), jnp.float32),
        pltpu.VMEM((count, LANES), jnp.float32),
        pltpu.VMEM((nx * ny * count, LANES), jnp.float32),
        pltpu.SemaphoreType.DMA((ndev,)),
        pltpu.SemaphoreType.DMA((ndev,)),
        pltpu.VMEM(fields.shape, jnp.float32),
        pltpu.SMEM(exponents.shape, jnp.int32),
        pltpu.VMEM(tables[0].shape, jnp.float32),
        pltpu.VMEM(tables[1].shape, jnp.float32),
        pltpu.SemaphoreType.DMA((4,)),
    ]
    vmem = pl.BlockSpec(memory_space=pltpu.VMEM)
    return pl.pallas_call(
        functools.partial(kernel, sizes, cells),
        out_shape=(
            jax.ShapeDtypeStruct(fields.shape, jnp.float32),
            jax.ShapeDtypeStruct((2, 1, LEVELS), jnp.float32),
        ),
        in_specs=[pl.BlockSpec(memory_space=pltpu.HBM)] * 4,
        out_specs=(vmem, vmem),
        scratch_shapes=scratch,
        compiler_params=pltpu.CompilerParams(
            collective_id=0, has_side_effects=True, vmem_limit_bytes=VMEM_LIMIT
        ),
    )(exponents, fields, *tables)


def solution(mesh):
    sizes = tuple(mesh.shape[name] for name in ("gx", "gy", "gz"))
    placed = (P(None, "gx", "gy", "gz"), P())
    return jax.shard_map(
        functools.partial(shards, sizes),
        mesh=mesh,
        in_specs=placed,
        out_specs=placed,
        check_vma=False,
    )
```

profile of v0, /device:TPU:0, one launch (start us, length us, event | category | flops | bytes accessed | tf_op | source)
XLA Modules:
  0.0 33.4 jit_solution(7430399102834669188)
XLA Ops:
  0.6 30.3 %shard_map.59 = (f32[1,32,32,128]{3,2,1,0:T(8,128)}, f32[2,1,5]{2,1,0:T(1,128)}) custom-call(s32[5]{0:T(128)} %exps_in.1, f32[1,32,32,128]{3,2,1,0:T(8,128)} %field_in.1, f32[2,128,128]{2,1,0:T(8,128)} %constant.4.clone.rows_in, f32[2,128,128]{2,1,0:T(8,128)} %constant.5.clone.lanes_in), custom_call_target="tpu_custom_call" | custom-call | tf_op jit(solution)/shard_map/pallas_call | solution.py:410
  30.9 0.0 copy-start
  31.0 1.9 %copy.8 = f32[1,32,32,128]{3,2,1,0:T(8,128)} copy(f32[1,32,32,128]{3,2,1,0:T(8,128)} %get-tuple-element.4) | data formatting | bytes 1048576
  32.8 0.0 copy-done
  32.8 0.6 %copy.9 = f32[2,1,5]{2,1,0:T(1,128)} copy(f32[2,1,5]{2,1,0:T(1,128)S(1)} %copy-done) | data formatting | bytes 80
Async XLA Ops:
  30.9 1.9 %copy-start = (f32[2,1,5]{2,1,0:T(1,128)S(1)}, f32[2,1,5]{2,1,0:T(1,128)}, u32[]{:S(2)}) copy-start(f32[2,1,5]{2,1,0:T(1,128)} %get-tuple-element.5) | copy-start | bytes 124
where the time goes:
time: 33.5 us; the launch traced here: 33.4 us
  Pallas kernels  30.3 us (90%)
  local copies, waits for them, and re-layouts  2.44 us (7%)
  between operations  0.65 us (2%)
    pallas_call x1, Pallas kernels, shards(): pl.pallas_call(functools.partial(kernel, sizes, cells), out_shape=(jax.Sh...  30.3 us
    unnamed x4, local copies, waits for them, and re-layouts  2.44 us

commit v1 on v0

--- a/solution.py
+++ b/solution.py
@@ -12,8 +12,9 @@
 FINE = 3
 LEVELS = 5
 LANES = 128
+CHUNKS = 4
 BUFFERS = 19
-VMEM_LIMIT = 67_043_328
+VMEM_LIMIT = 33_554_432
 MESH = pl.DeviceIdType.MESH
 
 
@@ -369,6 +370,18 @@
     for x in range(cx):
         spot = (0, step * x, pl.ds(0, cy, stride=step), slice(None))
         out[spot] = jnp.where(keep, rows_s[pl.ds(x * cy, cy), :], out[spot])
+
+
+def deliver(held, held_stats, out, stats, sem):
+    rows = held.shape[1] // CHUNKS
+    copies = [pltpu.make_async_copy(held_stats, stats, sem.at[CHUNKS])]
+    for i in range(CHUNKS):
+        part = pl.ds(i * rows, rows)
+        copies.append(pltpu.make_async_copy(held.at[:, part], out.at[:, part], sem.at[i]))
+    for copy in copies:
+        copy.start()
+    for copy in copies:
+        copy.wait()
 
 
 def shards(sizes, fields, exponents):
@@ -407,11 +420,11 @@
         pltpu.SemaphoreType.DMA((4,)),
     ]
     vmem = pl.BlockSpec(memory_space=pltpu.VMEM)
-    return pl.pallas_call(
+    held = pl.pallas_call(
         functools.partial(kernel, sizes, cells),
         out_shape=(
-            jax.ShapeDtypeStruct(fields.shape, jnp.float32),
-            jax.ShapeDtypeStruct((2, 1, LEVELS), jnp.float32),
+            pltpu.VMEM(fields.shape, jnp.float32),
+            pltpu.VMEM((2, 1, LEVELS), jnp.float32),
         ),
         in_specs=[pl.BlockSpec(memory_space=pltpu.HBM)] * 4,
         out_specs=(vmem, vmem),
@@ -419,7 +432,18 @@
         compiler_params=pltpu.CompilerParams(
             collective_id=0, has_side_effects=True, vmem_limit_bytes=VMEM_LIMIT
         ),
-    )(exponents, fields, *tables)
+    )(*(pltpu.with_memory_space_constraint(x, pltpu.HBM) for x in (exponents, fields, *map(jnp.asarray, tables))))
+    hbm = pl.BlockSpec(memory_space=pltpu.HBM)
+    return pl.pallas_call(
+        deliver,
+        out_shape=(
+            jax.ShapeDtypeStruct(fields.shape, jnp.float32),
+            jax.ShapeDtypeStruct((2, 1, LEVELS), jnp.float32),
+        ),
+        in_specs=(vmem, vmem),
+        out_specs=(hbm, hbm),
+        scratch_shapes=[pltpu.SemaphoreType.DMA((CHUNKS + 1,))],
+    )(*(pltpu.with_memory_space_constraint(x, pltpu.VMEM) for x in held))
 
 
 def solution(mesh):

time: 33.5 us -> 31.1 us (0.928)
  local copies, waits for them, and re-layouts: 2.44 us -> 0 us
    unnamed x4 -> x0, local copies, waits for them, and re-layouts: 2.44 us -> none
    pallas_call x1 -> x2, Pallas kernels: 30.3 us -> 30.4 us  [the longest x1 29.5 us: shards(): pl.pallas_call(functools.partial(kernel, sizes, cells), out_shape=(pltpu....]
where the time goes in v1:
time: 31.1 us; the launch traced here: 31 us
  Pallas kernels  30.4 us (98%)
  between operations  0.64 us (2%)
    pallas_call x1, Pallas kernels, shards(): pl.pallas_call(functools.partial(kernel, sizes, cells), out_shape=(pltpu....  29.5 us
    pallas_call x1, Pallas kernels, shards(): pl.pallas_call(deliver, out_shape=(jax.ShapeDtypeStruct(fields.shape, jnp...  0.83 us

profile of v1, /device:TPU:0, one launch (start us, length us, event | category | flops | bytes accessed | tf_op | source)
XLA Modules:
  0.0 31.0 jit_solution(15111001203986495042)
XLA Ops:
  0.6 29.5 %shard_map.59 = (f32[1,32,32,128]{3,2,1,0:T(8,128)S(1)}, f32[2,1,5]{2,1,0:T(1,128)S(1)}) custom-call(s32[5]{0:T(128)} %exps_in.1, f32[1,32,32,128]{3,2,1,0:T(8,128)} %field_in.1, f32[2,128,128]{2,1,0:T(8,128)} %constant.4.clone.rows_in, f32[2,128,128]{2,1,0:T(8,128)} %constant.5.clone.lanes_in), custom_call_target="tpu_custom_call" | custom-call | tf_op jit(solution)/shard_map/pallas_call | solution.py:423
  30.2 0.8 %shard_map.60 = (f32[1,32,32,128]{3,2,1,0:T(8,128)}, f32[2,1,5]{2,1,0:T(1,128)}) custom-call(f32[1,32,32,128]{3,2,1,0:T(8,128)S(1)} %get-tuple-element.4.held, f32[2,1,5]{2,1,0:T(1,128)S(1)} %get-tuple-element.5.held_stats), custom_call_target="tpu_custom_call" | custom-call | tf_op jit(solution)/shard_map/pallas_call | solution.py:437

commit v2 on v1

v2 whole, which is shorter than its diff:
```python
import functools

import numpy as np

import jax
import jax.numpy as jnp
from jax import lax
from jax.experimental import pallas as pl
from jax.experimental.pallas import tpu as pltpu
from jax.sharding import PartitionSpec as P

FINE = 3
LEVELS = 5
LANES = 128
CHUNKS = 4
BUFFERS = 18
TABLES = 7
ROUNDS = 2
VMEM_LIMIT = 33_554_432
MESH = pl.DeviceIdType.MESH


def periodic_lift(length):
    eye = np.eye(length)
    even, odd = eye[0::2], eye[1::2]
    detail = odd - 0.5 * (even + np.roll(even, -1, 0))
    smooth = even + 0.25 * (np.roll(detail, 1, 0) + detail)
    whole = np.zeros((length, length))
    whole[0::2] = smooth
    whole[1::2] = detail
    return whole


def second_lift(length):
    whole = np.zeros((length, length))
    whole[0::2, 0::2] = periodic_lift(length // 2)
    return whole


def coarse_matrices(sizes, coarse):
    nx, ny, nz = sizes
    cx, cy, cz = coarse
    rows = np.arange(nx * ny * cx * cy)
    dev, inner = rows // (cx * cy), rows % (cx * cy)
    gx = (dev // ny) * cx + inner // cy
    gy = (dev % ny) * cy + inner % cy
    step = LANES // cz
    lanes = np.array([z * step + d for d in range(nz) for z in range(cz)])
    result = []
    for both_levels in (False, True):
        mx, my, mz = periodic_lift(nx * cx), periodic_lift(ny * cy), periodic_lift(nz * cz)
        if both_levels:
            mx, my, mz = second_lift(nx * cx) @ mx, second_lift(ny * cy) @ my, second_lift(nz * cz) @ mz
        both = mx[gx[:, None], gx[None]] * my[gy[:, None], gy[None]]
        along = np.zeros((LANES, LANES))
        along[np.ix_(lanes, lanes)] = mz.T
        result.append((both.astype(np.float32), along.astype(np.float32)))
    return [np.stack(pair) for pair in zip(*result)]


def lift_line(n):
    whole = np.zeros((n, n + 2))
    cells = np.eye(n + 2)
    even, odd = cells[0:n:2], cells[1:n:2]
    after = np.concatenate((even[1:], cells[n + 1 :]))
    detail = odd - 0.5 * (even + after)
    before = np.concatenate((cells[n : n + 1] - 0.5 * even[:1], detail[:-1]))
    whole[0::2] = even + 0.25 * (before + detail)
    whole[1::2] = detail
    return whole

def line_tables(n):
    lift = lift_line(n)
    own = lift[:, :n]
    sent = np.zeros((4, n))
    sent[0, n - 1], sent[0, n - 2] = 1.0, -0.5
    sent[1] = own[n - 2] - 0.5 * own[n - 4]
    sent[2, 0] = 1.0
    sent[3] = own[0]
    first = np.zeros((n + 2, n + 4))
    first[:n, :n] = own
    first[:n, n], first[:n, n + 2] = lift[:, n], lift[:, n + 1]
    first[n, n + 1], first[n, 0] = 1.0, lift[n - 2, n + 1]
    first[n + 1, n + 3] = 1.0
    first[n + 1, :n] = lift[0, n] * sent[0]
    return sent, first, lift_line(n // 2)


def middle_tables(ax, ay, az):
    step = LANES // az
    sent_x, first_x, second_x = line_tables(ax)
    sent_y, first_y, second_y = line_tables(ay)
    sent_z, first_z, second_z = line_tables(az)
    own = [(x, y) for x in range(ax) for y in range(ay)]
    corners = [(x, 2 * g + y) for g in range(2) for x in range(4) for y in range(2)]
    extra = [(ax + k, y) for k in range(4) for y in range(ay)]
    extra += [(x, ay + k) for k in range(4) for x in range(ax)]
    extra += [(ax + x, ay + y) for x, y in corners]
    taken = np.array(own + extra)
    given = own + [(ax + k, y) for k in range(2) for y in range(0, ay, 2)]
    given += [(x, ay + k) for k in range(2) for x in range(0, ax, 2)]
    given += [(ax + x, ay + y) for x in range(2) for y in range(2)]
    height = -(-len(given) // 16) * 16

    whole_x, whole_y = np.concatenate((np.eye(ax), sent_x)), np.concatenate((np.eye(ay), sent_y))
    ex, ey = np.array(extra).T
    ox, oy = np.array(own).T
    send_rows = whole_x[np.ix_(ex, ox)] * whole_y[np.ix_(ey, oy)]
    gx, gy = np.array(given).T
    tx, ty = taken.T
    rows = np.zeros((height, len(taken)))
    rows[: len(given)] = first_x[np.ix_(gx, tx)] * first_y[np.ix_(gy, ty)]

    def spot(at, n):
        return np.where(at >= n, n // 2 + at - n, at // 2)

    half = np.array([(x, y) for x in range(ax // 2) for y in range(ay // 2)])
    use = ((gx % 2 == 0) | (gx >= ax)) & ((gy % 2 == 0) | (gy >= ay))
    last = np.zeros((len(half), height))
    pick_x = second_x[np.ix_(half[:, 0], spot(gx, ax))]
    pick_y = second_y[np.ix_(half[:, 1], spot(gy, ay))]
    last[:, : len(given)] = pick_x * pick_y * use

    lanes = np.arange(az) * step
    out = np.concatenate((lanes, [1, step + 1]))
    send_lanes = np.zeros((8, LANES))
    send_lanes[np.ix_(np.arange(4), lanes)] = sent_z
    along = np.zeros((LANES, LANES))
    along[np.ix_(lanes, out)] = first_z[:, :az].T
    rim = np.zeros((16, LANES))
    for part in range(3):
        rim[np.ix_(4 * part + np.arange(4), out)] = first_z[:, az:].T
    along_last = np.zeros((LANES, LANES))
    source = np.concatenate((lanes[0::2], [1, step + 1]))
    along_last[np.ix_(source, lanes[0::2])] = second_z.T
    result = (send_rows, rows, last, send_lanes, along, rim, along_last)
    return tuple(table.astype(jnp.bfloat16) for table in result)


def iota(shape, axis):
    return lax.broadcasted_iota(jnp.int32, shape, axis)


def roll(values, shift, axis):
    return pltpu.roll(values, shift % values.shape[axis], axis)


def lift_rows(v, low, high):
    n = v.shape[0]
    row = iota(v.shape, 0)
    odd = row % 2 == 1
    up = jnp.where(row == n - 1, high, roll(v, -1, 0))
    w = jnp.where(odd, v - 0.5 * (roll(v, 1, 0) + up), v)
    down = jnp.where(row == 0, low - 0.5 * v, roll(w, 1, 0))
    return jnp.where(odd, w, w + 0.25 * (down + roll(w, -1, 0)))


def lift_lanes(v, rim, s):
    lane = iota(v.shape, 1)
    up = jnp.where(lane == LANES - s, rim, roll(v, -s, 1))
    w = jnp.where(lane % (2 * s) == s, v - 0.5 * (roll(v, s, 1) + up), v)
    down = jnp.where(lane == 0, rim - 0.5 * v, roll(w, s, 1))
    return jnp.where(lane % (2 * s) == 0, w + 0.25 * (down + roll(w, -s, 1)), w)


def shrink(v, thresh):
    return v - jnp.clip(v, -thresh, thresh)


def three(v):
    parts = []
    for _ in range(3):
        parts.append(v.astype(jnp.bfloat16))
        v = v - parts[-1].astype(jnp.float32)
    return parts


def mix(a, b, dims):
    return lax.dot_general(a, b, (dims, ((), ())), preferred_element_type=jnp.float32)


def mix_rows(table, v):
    return sum(mix(table, part, ((1,), (0,))) for part in three(v))


def mix_lanes(v, table):
    return sum(mix(part, table, ((1,), (0,))) for part in three(v))


def total(v):
    return jnp.sum(jnp.sum(v, axis=0, keepdims=True), axis=1, keepdims=True)


def kernel(sizes, cells, exps_in, field_in, rows_in, lanes_in, *rest):
    tables_in, (out, stats), scratch = rest[:TABLES], rest[TABLES : TABLES + 2], rest[TABLES + 2 :]
    nx, ny, nz = sizes
    ndev = nx * ny * nz
    scratch = list(scratch)
    tables = scratch[-TABLES:]
    scratch = scratch[:-TABLES]
    field, exps, k_s, l_s, in_sem = scratch[-5:]
    scratch = scratch[:-5]
    pairs = [(field_in, field), (exps_in, exps), *zip(tables_in, tables), (rows_in, k_s), (lanes_in, l_s)]
    loads = [pltpu.make_async_copy(a, b, in_sem.at[i]) for i, (a, b) in enumerate(pairs)]
    for load in loads:
        load.start()
    me = (lax.axis_index("gx"), lax.axis_index("gy"), lax.axis_index("gz"))

    def device(dx, dy, dz):
        return (
            lax.rem(me[0] + (dx + nx), nx),
            lax.rem(me[1] + (dy + ny), ny),
            lax.rem(me[2] + (dz + nz), nz),
        )

    def thresh(level):
        return jnp.exp2(jnp.full((1, LANES), exps[level].astype(jnp.float32)))

    def split(j):
        return j // (ny * nz), (j // nz) % ny, j % nz

    barrier = pltpu.get_barrier_semaphore()

    near = max(sizes) // 2 <= ROUNDS
    greeted = {
        tuple((d + size - 1) % size if near else d for d, size in zip(spot, sizes))
        for spot in np.ndindex(*(3, 3, 3) if near else sizes)
    } - {(0, 0, 0)}
    for spot in sorted(greeted):
        pl.semaphore_signal(barrier, inc=1, device_id=device(*spot), device_id_type=MESH)
    gath, msg, rows_s, final_s, g_send, g_recv = scratch[-6:]
    loads[0].wait()
    loads[1].wait()
    away = (-1, 1)
    alone = nx == 2

    (xs, xr, ys, yr, es, er, yl, zs, zr, hs, hr, ds, dr, cs, cr, work, send_sem, recv_sem) = scratch[:BUFFERS]
    grown, sent, rims, side, hz, t2r, t3r, o1s, o2s, m_send, m_recv = scratch[BUFFERS : BUFFERS + 11]
    s = 1
    n = field.shape[2] // s
    px = field.shape[1] // s
    src = field.at[0]
    lane = iota((n, LANES), 1)

    def edge(v):
        return v[0:1], v[n - 1 : n] - 0.5 * v[n - 2 : n - 1]

    e_plane = src[0]
    p_plane = src[px - 1] - 0.5 * src[px - 2]
    xs[0] = e_plane
    xs[1] = p_plane
    ys[0] = src[:, 0, :]
    ys[1] = src[:, n - 1, :] - 0.5 * src[:, n - 2, :]
    for a, plane in ((0, e_plane), (1, p_plane)):
        es[2 * a], es[2 * a + 1] = edge(plane)

    packed = jnp.zeros((n, LANES), jnp.float32)
    for x in range(px):
        v = src[x]
        u = jnp.where(lane == LANES - s, v - 0.5 * roll(v, s, 1), v)
        at = 2 * s * x
        packed = jnp.where((lane == at) | (lane == at + s), roll(u, at + s, 1), packed)
    half = 2 * s * px
    combined = packed - 0.5 * roll(packed, 2 * s, 1)
    sides = roll(jnp.where(lane < half // 2, packed, combined), half, 1)
    zs[...] = packed
    hs[...] = sides
    ds[0], ds[1] = edge(packed)
    cs[0], cs[1] = edge(sides)

    pl.semaphore_wait(barrier, len(greeted))
    copies = []
    ways = (0,) if alone else (0, 1)
    for i in (0, 1):
        for b in (0, 1):
            for a in ways:
                copies.append((cs.at[b], cr.at[4 * a + 2 * b + i], (away[a], away[b], away[i])))
            copies.append((ds.at[b], dr.at[2 * b + i], (0, away[b], away[i])))
    for a in (0, 1):
        for b in (0, 1):
            copies.append((es.at[2 * a + b], er.at[2 * a + b], (away[a], away[b], 0)))
    for b in (0, 1):
        copies.append((ys.at[b], yr.at[b], (0, away[b], 0)))
    for i in (0, 1):
        for a in ways:
            copies.append((hs, hr.at[2 * a + i], (away[a], 0, away[i])))
    for a in (0, 1):
        copies.append((xs.at[a], xr.at[a], (away[a], 0, 0)))
    for i in (0, 1):
        copies.append((zs, zr.at[i], (0, 0, away[i])))
    flights = [
        pltpu.make_async_remote_copy(
            src_ref=f, dst_ref=t, send_sem=send_sem.at[i], recv_sem=recv_sem.at[i],
            device_id=device(*d), device_id_type=MESH,
        )
        for i, (f, t, d) in enumerate(copies)
    ]
    for flight in flights:
        flight.start()
    for flight in flights:
        flight.wait()

    for b in (0, 1):
        yl[b] = lift_rows(yr[b], er[2 + b], er[b])

    def rim_of(main, side):
        spot = iota(main(0).shape, 1)
        parts = []
        for i in (0, 1):
            after = side(0, i)
            before = after if alone else side(1, i)
            v = jnp.where(spot < half, main(i), 0.0)
            v = jnp.where((spot >= half) & (spot < half + 2 * s), after, v)
            parts.append(jnp.where(spot >= LANES - 2 * s, before, v))
        v = jnp.where(spot % (2 * s) < s, roll(parts[0], -s, 1), roll(parts[1], s, 1))
        odd = (spot // (2 * s)) % 2 == 1
        w = jnp.where(odd, v - 0.5 * (roll(v, 2 * s, 1) + roll(v, -2 * s, 1)), v)
        return jnp.where(odd, w, w + 0.25 * (roll(w, 2 * s, 1) + roll(w, -2 * s, 1)))

    rim_rows = [
        rim_of(lambda i: dr[2 * b + i], lambda a, i: cr[4 * a + 2 * b + i]) for b in (0, 1)
    ]
    rim = rim_of(lambda i: zr[i], lambda a, i: hr[2 * a + i])
    rim = lift_rows(rim, rim_rows[1], rim_rows[0])
    level_thresh = thresh(0)
    inner = (lane % (2 * s) == 0) & (iota((n, LANES), 0) % 2 == 0)

    def plane_step(x, v):
        v = lift_rows(v, yl[1, x : x + 1, :], yl[0, x : x + 1, :])
        v = lift_lanes(v, roll(rim, LANES - s - 2 * s * x, 1), s)
        work[x] = v
        if x % 2 == 0:
            grown[pl.ds(x // 2 * (n // 2), n // 2), :] = work[x, pl.ds(0, n // 2, stride=2), :]

    def finish():
        energy = kept = jnp.zeros((n, LANES), jnp.float32)
        for x in range(px):
            v = work[x]
            small = shrink(v, level_thresh)
            if x % 2 == 0:
                energy += jnp.where(inner, 0.0, v * v)
                kept += jnp.where(inner, 0.0, jnp.abs(small))
            else:
                energy += v * v
                kept += jnp.abs(small)
            out[0, x] = small
        return [total(energy), total(kept)]

    even = src[0]
    before = xr[1] - 0.5 * even
    for k in range(px // 2):
        after = src[2 * k + 2] if 2 * k + 2 < px else xr[0]
        detail = src[2 * k + 1] - 0.5 * (even + after)
        smooth = even + 0.25 * (before + detail)
        plane_step(2 * k, smooth)
        plane_step(2 * k + 1, detail)
        even, before = after, detail

    ax, ay = px // 2, n // 2
    own = ax * ay
    send_rows, rows1, rows2, send_lanes, lanes1, rim1, lanes2 = tables
    for load in loads[2 : 2 + TABLES]:
        load.wait()
    here = grown[0:own]
    halo = mix_rows(send_rows[...], here)
    sent[...] = halo
    edges = sum(
        mix(send_lanes[...], part, ((1,), (1,)))
        for part in three(jnp.concatenate((here, halo), axis=0))
    )
    extra = halo.shape[0]
    for g in (0, 1):
        side[g, :, pl.ds(own, 2 * LANES)] = jnp.zeros((2, 2 * LANES), jnp.float32)
        side[g, :, pl.ds(0, own + extra)] = edges[2 * g : 2 * g + 2]

    step_to = (1, -1)
    px_rows, py_rows = 4 * ay, 4 * ax
    copies = []
    for g in (0, 1):
        dz = step_to[g]
        tail = pl.ds(own + LANES, LANES)
        for gy in (0, 1):
            for gx in ways:
                copies.append((side.at[g, :, tail], t3r.at[g, gy, gx], (step_to[gx], step_to[gy], dz)))
        middle = pl.ds(own, LANES)
        for gx in ways:
            copies.append((side.at[g, :, middle], t2r.at[g, gx], (step_to[gx], 0, dz)))
        for gy in (0, 1):
            copies.append((side.at[g, :, middle], t2r.at[g, 2 + gy], (0, step_to[gy], dz)))
        copies.append((side.at[g, :, pl.ds(0, own)], hz.at[g, :, pl.ds(0, own)], (0, 0, dz)))

    def rows_copy(start, size, to):
        copies.append((sent.at[pl.ds(start, size)], grown.at[pl.ds(own + start, size)], to))

    parts = len(ways)
    for gy in (0, 1):
        for gx in ways:
            rows_copy(px_rows + py_rows + 8 * gy + 4 * gx, 8 // parts, (step_to[gx], step_to[gy], 0))
    for gx in ways:
        rows_copy(px_rows // 2 * gx, px_rows // parts, (step_to[gx], 0, 0))
    for gy in (0, 1):
        rows_copy(px_rows + py_rows // 2 * gy, py_rows // 2, (0, step_to[gy], 0))
    flights = [
        pltpu.make_async_remote_copy(
            src_ref=f, dst_ref=t, send_sem=m_send.at[i], recv_sem=m_recv.at[i],
            device_id=device(*d), device_id_type=MESH,
        )
        for i, (f, t, d) in enumerate(copies)
    ]
    for flight in flights:
        flight.start()
    sums = finish()
    for flight in flights:
        flight.wait()

    lane2 = iota((2, LANES), 1)
    for g in (0, 1):
        v = jnp.where(lane2 < px_rows // 2, t2r[g, 0], t2r[g, 0 if alone else 1])
        v = jnp.where(lane2 < px_rows, v, jnp.where(lane2 < px_rows + py_rows // 2, t2r[g, 2], t2r[g, 3]))
        hz[g, :, pl.ds(own, LANES)] = v
        u = []
        for gy in (0, 1):
            u.append(jnp.where(lane2 % 8 < 4, t3r[g, gy, 0], t3r[g, gy, 0 if alone else 1]))
        v = jnp.where(lane2 < 8, u[0], u[1])
        hz[g, :, pl.ds(own + LANES, LANES)] = jnp.where(lane2 < 16, v, 0.0)
    pieces = []
    for part in three(jnp.concatenate((hz[0], hz[1]), axis=0)):
        pieces.append(part.astype(jnp.float32))
    pieces.append(jnp.zeros_like(pieces[0]))
    rim_rows = mix(jnp.concatenate(pieces, axis=0).astype(jnp.bfloat16), rim1[...], ((0,), (0,)))
    wide = mix_lanes(grown[...], lanes1[...]) + rim_rows[0 : own + extra]
    first = mix_rows(rows1[...], wide)
    second = mix_lanes(mix_rows(rows2[...], first), lanes2[...])
    o1s[...] = first[0:own]
    o2s[...] = second.reshape(o2s.shape)

    def tally(v, level, ny):
        s = 2**level
        row, at = iota(v.shape, 0), iota(v.shape, 1)
        smooth = ((row // ny) % 2 == 0) & (row % 2 == 0) & (at % (2 * s) == 0)
        use = (at % s == 0) & ~smooth
        small = shrink(v, thresh(level))
        return [total(jnp.where(use, v * v, 0.0)), total(jnp.where(use, jnp.abs(small), 0.0))]

    sums += tally(first[0:own], 1, ay) + tally(second, 2, ay // 2)

    def place(source, level):
        s = 2**level
        small_y = ay >> (level - 1)
        keep = iota((small_y, LANES), 1) % s == 0
        for x in range(ax >> (level - 1)):
            spot = (0, s * x, pl.ds(0, small_y, stride=s), slice(None))
            out[spot] = jnp.where(keep, shrink(source(x), thresh(level)), out[spot])

    cx, cy = ax // 4, ay // 4
    step = 2**FINE
    count = cx * cy
    for x in range(cx):
        rows_s[pl.ds(x * cy, cy), :] = o2s[2 * x, pl.ds(0, cy, stride=2), :]
    here = rows_s[...]
    lane = iota((count, LANES), 1)
    row = iota((count, LANES), 0)
    here = jnp.where(lane % step == 0, here, 0.0)
    for bit in (1, 2, 4):
        here = jnp.where((row & bit) != 0, roll(here, bit, 1), here)
    groups = count // 8
    one = iota((1, LANES), 1)
    for g in range(groups):
        msg[g : g + 1] = jnp.sum(here[8 * g : 8 * g + 8], axis=0, keepdims=True)
    tail = jnp.zeros((1, LANES), jnp.float32)
    for i, whole in enumerate(sums):
        tail = jnp.where(one == i, whole, tail)
    msg[groups:] = jnp.broadcast_to(tail, (msg.shape[0] - groups, LANES))
    flat = (me[0] * ny + me[1]) * nz + me[2]

    def post(j):
        return pltpu.make_async_remote_copy(
            src_ref=msg, dst_ref=gath.at[flat], send_sem=g_send.at[j], recv_sem=g_recv.at[j],
            device_id=device(*split(j)), device_id_type=MESH,
        )

    def send(j, carry):
        post(ndev - j).start()
        return carry

    def settle(j, carry):
        post(j).wait()
        return carry

    def place_all():
        place(lambda x: o1s[pl.ds(x * ay, ay), :], 1)
        place(lambda x: o2s[x], 2)

    if ndev <= 32:
        posts = [post(ndev - j) for j in range(1, ndev)]
        for flight in posts:
            flight.start()
        gath[flat] = msg[...]
        place_all()
        for flight in posts:
            flight.wait()
    else:
        lax.fori_loop(1, ndev, send, 0)
        gath[flat] = msg[...]
        place_all()
        lax.fori_loop(1, ndev, settle, 0)

    sub = iota((8, LANES), 0)
    lane8 = iota((8, LANES), 1)

    def unpack(d, tail):
        for g in range(groups):
            acc = jnp.zeros((8, LANES), jnp.float32)
            for z in range(nz):
                v = jnp.broadcast_to(gath[d * nz + z, g : g + 1, :], (8, LANES))
                for bit in (1, 2, 4):
                    v = jnp.where((sub & bit) != 0, roll(v, -bit, 1), v)
                acc += roll(jnp.where(lane8 % step == 0, v, 0.0), z, 1)
            final_s[pl.ds(pl.multiple_of(d * count + 8 * g, 8), 8), :] = acc
        for z in range(nz):
            tail += gath[d * nz + z, groups : groups + 1, :]
        return tail

    tail = lax.fori_loop(0, nx * ny, unpack, jnp.zeros((1, LANES), jnp.float32), unroll=nx * ny <= 8)

    def dot(a, b):
        return jnp.dot(a, b, precision=lax.Precision.HIGHEST, preferred_element_type=jnp.float32)

    grid = final_s[...]
    loads[2 + TABLES].wait()
    loads[3 + TABLES].wait()
    half3, half4 = dot(k_s[0], grid), dot(k_s[1], grid)
    grid, grid4 = dot(half3, l_s[0]), dot(half4, l_s[1])
    row = iota(grid.shape, 0)
    lane = iota(grid.shape, 1)
    inner_row = row % count
    gx, gy, gz = inner_row // cy, inner_row % cy, lane // step
    valid = lane % step < nz
    even3 = (gx % 2 == 0) & (gy % 2 == 0) & (gz % 2 == 0)
    even4 = (gx % 4 == 0) & (gy % 4 == 0) & (gz % 4 == 0)
    det3 = valid & ~even3
    det4 = valid & even3 & ~even4
    small3 = shrink(grid, thresh(FINE))
    small4 = shrink(grid4, thresh(FINE + 1))
    final_s[...] = jnp.where(even3, jnp.where(even4, grid4, small4), small3)

    def masked(mask, v):
        return total(jnp.where(mask, v, 0.0))

    coarse = ((masked(det3, grid * grid), masked(det3, jnp.abs(small3))),
              (masked(det4, grid4 * grid4), masked(det4, jnp.abs(small4))))
    for q in (0, 1):
        line = jnp.zeros((1, LANES), jnp.float32)
        for level in range(LEVELS):
            weight = 8.0 ** (level + 1) / (7.0 * cells)
            if level < FINE:
                value = jnp.sum(jnp.where(one == 2 * level + q, tail, 0.0), axis=1, keepdims=True)
            else:
                value = coarse[level - FINE][q]
            line = jnp.where(one == level, value * weight, line)
        stats[q] = line[:, 0:LEVELS]

    first = pl.multiple_of((me[0] * ny + me[1]) * count, count)
    mine = pltpu.roll(final_s[pl.ds(first, count), :], lax.rem(LANES - me[2], LANES), 1)
    rows_s[...] = mine
    keep = iota((cy, LANES), 1) % step == 0
    for x in range(cx):
        spot = (0, step * x, pl.ds(0, cy, stride=step), slice(None))
        out[spot] = jnp.where(keep, rows_s[pl.ds(x * cy, cy), :], out[spot])


def deliver(held, held_stats, out, stats, sem):
    rows = held.shape[1] // CHUNKS
    copies = [pltpu.make_async_copy(held_stats, stats, sem.at[CHUNKS])]
    for i in range(CHUNKS):
        part = pl.ds(i * rows, rows)
        copies.append(pltpu.make_async_copy(held.at[:, part], out.at[:, part], sem.at[i]))
    for copy in copies:
        copy.start()
    for copy in copies:
        copy.wait()


def shards(sizes, fields, exponents):
    nx, ny, nz = sizes
    ndev = nx * ny * nz
    _, lx, ly, lz = fields.shape
    cells = fields.size * ndev
    step = 2**FINE
    coarse = (lx // step, ly // step, lz // step)
    count = coarse[0] * coarse[1]
    tables = coarse_matrices(sizes, coarse)
    middle = middle_tables(lx // 2, ly // 2, lz // 2)
    own, extra = lx // 2 * (ly // 2), middle[0].shape[0]
    scratch = [
        *(pltpu.VMEM(shape, jnp.float32) for shape in (
            (2, ly, LANES), (2, ly, LANES), (2, lx, LANES), (2, lx, LANES), (4, 1, LANES), (4, 1, LANES),
            (2, lx, LANES), (ly, LANES), (2, ly, LANES), (ly, LANES), (4, ly, LANES), (2, 1, LANES),
            (4, 1, LANES), (2, 1, LANES), (8, 1, LANES), (lx, ly, LANES),
        )),
        pltpu.SemaphoreType.DMA((26,)),
        pltpu.SemaphoreType.DMA((26,)),
        *(pltpu.VMEM(shape, jnp.float32) for shape in (
            (own + extra, LANES), (extra, LANES), (1, LANES), (2, 2, own + 2 * LANES), (2, 2, own + 2 * LANES),
            (2, 4, 2, LANES), (2, 2, 2, 2, LANES), (own, LANES), (lx // 4, ly // 4, LANES),
        )),
        pltpu.SemaphoreType.DMA((26,)),
        pltpu.SemaphoreType.DMA((26,)),
    ]
    height = -(-(count // 8 + 1) // 4) * 4
    scratch += [
        pltpu.VMEM((ndev, height, LANES), jnp.float32),
        pltpu.VMEM((height, LANES), jnp.float32),
        pltpu.VMEM((count, LANES), jnp.float32),
        pltpu.VMEM((nx * ny * count, LANES), jnp.float32),
        pltpu.SemaphoreType.DMA((ndev,)),
        pltpu.SemaphoreType.DMA((ndev,)),
        pltpu.VMEM(fields.shape, jnp.float32),
        pltpu.SMEM(exponents.shape, jnp.int32),
        pltpu.VMEM(tables[0].shape, jnp.float32),
        pltpu.VMEM(tables[1].shape, jnp.float32),
        pltpu.SemaphoreType.DMA((4 + TABLES,)),
        *(pltpu.VMEM(table.shape, table.dtype) for table in middle),
    ]
    vmem = pl.BlockSpec(memory_space=pltpu.VMEM)
    held = pl.pallas_call(
        functools.partial(kernel, sizes, cells),
        out_shape=(
            pltpu.VMEM(fields.shape, jnp.float32),
            pltpu.VMEM((2, 1, LEVELS), jnp.float32),
        ),
        in_specs=[pl.BlockSpec(memory_space=pltpu.HBM)] * (4 + TABLES),
        out_specs=(vmem, vmem),
        scratch_shapes=scratch,
        compiler_params=pltpu.CompilerParams(
            collective_id=0, has_side_effects=True, vmem_limit_bytes=VMEM_LIMIT
        ),
    )(*(pltpu.with_memory_space_constraint(x, pltpu.HBM) for x in (exponents, fields, *map(jnp.asarray, (*tables, *middle)))))
    hbm = pl.BlockSpec(memory_space=pltpu.HBM)
    return pl.pallas_call(
        deliver,
        out_shape=(
            jax.ShapeDtypeStruct(fields.shape, jnp.float32),
            jax.ShapeDtypeStruct((2, 1, LEVELS), jnp.float32),
        ),
        in_specs=(vmem, vmem),
        out_specs=(hbm, hbm),
        scratch_shapes=[pltpu.SemaphoreType.DMA((CHUNKS + 1,))],
    )(*(pltpu.with_memory_space_constraint(x, pltpu.VMEM) for x in held))


def solution(mesh):
    sizes = tuple(mesh.shape[name] for name in ("gx", "gy", "gz"))
    placed = (P(None, "gx", "gy", "gz"), P())
    return jax.shard_map(
        functools.partial(shards, sizes),
        mesh=mesh,
        in_specs=placed,
        out_specs=placed,
        check_vma=False,
    )
```

time: 31.1 us -> 27.6 us (0.89)
  Pallas kernels: 30.4 us -> 26.8 us
    pallas_call x1, Pallas kernels: 29.5 us -> 26 us  [shards(): pl.pallas_call(functools.partial(kernel, sizes, cells), out_shape=(pltpu....]
where the time goes in v2:
time: 27.6 us; the launch traced here: 27.5 us
  Pallas kernels  26.8 us (97%)
  between operations  0.64 us (2%)
    pallas_call x1, Pallas kernels, shards(): pl.pallas_call(functools.partial(kernel, sizes, cells), out_shape=(pltpu....  26 us
    pallas_call x1, Pallas kernels, shards(): pl.pallas_call(deliver, out_shape=(jax.ShapeDtypeStruct(fields.shape, jnp...  0.83 us

profile of v2, /device:TPU:0, one launch (start us, length us, event | category | flops | bytes accessed | tf_op | source)
XLA Modules:
  0.0 27.5 jit_solution(16657545939723726215)
XLA Ops:
  0.6 26.0 %shard_map.122 = (f32[1,32,32,128]{3,2,1,0:T(8,128)S(1)}, f32[2,1,5]{2,1,0:T(1,128)S(1)}) custom-call(s32[5]{0:T(128)} %exps_in.1, f32[1,32,32,128]{3,2,1,0:T(8,128)} %field_in.1, f32[2,128,128]{2,1,0:T(8,128)} %constant.18.clone.rows_in, f32[2,128,128]{2,1,0:T(8,128)} %constant.19.clone.lanes_in, bf16[144,256]{1,0:T(8,128)(2,1)} %constant.20.clone.rest_0_, ...), custom_call_target="tpu_custom_call" | custom-call | tf_op jit(solution)/shard_map/pallas_call | solution.py:626
  26.6 0.8 %shard_map.123 = (f32[1,32,32,128]{3,2,1,0:T(8,128)}, f32[2,1,5]{2,1,0:T(1,128)}) custom-call(f32[1,32,32,128]{3,2,1,0:T(8,128)S(1)} %get-tuple-element.4.held, f32[2,1,5]{2,1,0:T(1,128)S(1)} %get-tuple-element.5.held_stats), custom_call_target="tpu_custom_call" | custom-call | tf_op jit(solution)/shard_map/pallas_call | solution.py:640

commit v3 on v2

--- a/solution.py
+++ b/solution.py
@@ -46,6 +46,7 @@
     gy = (dev % ny) * cy + inner % cy
     step = LANES // cz
     lanes = np.array([z * step + d for d in range(nz) for z in range(cz)])
+    order = np.arange(nx * ny * cx * cy).reshape(nx * ny, -1, 8).transpose(2, 1, 0).reshape(-1)
     result = []
     for both_levels in (False, True):
         mx, my, mz = periodic_lift(nx * cx), periodic_lift(ny * cy), periodic_lift(nz * cz)
@@ -54,7 +55,7 @@
         both = mx[gx[:, None], gx[None]] * my[gy[:, None], gy[None]]
         along = np.zeros((LANES, LANES))
         along[np.ix_(lanes, lanes)] = mz.T
-        result.append((both.astype(np.float32), along.astype(np.float32)))
+        result.append((both[:, order].astype(np.float32), along.astype(np.float32)))
     return [np.stack(pair) for pair in zip(*result)]
 
 
@@ -180,11 +181,12 @@
 
 
 def mix_rows(table, v):
-    return sum(mix(table, part, ((1,), (0,))) for part in three(v))
+    wide = mix(table, jnp.concatenate(three(v), axis=1), ((1,), (0,)))
+    return wide[:, :LANES] + wide[:, LANES : 2 * LANES] + wide[:, 2 * LANES :]
 
 
 def mix_lanes(v, table):
-    return sum(mix(part, table, ((1,), (0,))) for part in three(v))
+    return mix(jnp.concatenate(three(v), axis=1), jnp.concatenate([table] * 3, axis=0), ((1,), (0,)))
 
 
 def total(v):
@@ -219,6 +221,22 @@
     def split(j):
         return j // (ny * nz), (j // nz) % ny, j % nz
 
+    def launch(copies, send_sem, recv_sem):
+        flights = [
+            pltpu.make_async_remote_copy(
+                src_ref=f, dst_ref=t, send_sem=send_sem, recv_sem=recv_sem,
+                device_id=device(*d), device_id_type=MESH,
+            )
+            for f, t, d in copies
+        ]
+        for flight in flights:
+            flight.start()
+        return sum(t.size for _, t, _ in copies) // LANES
+
+    def settle(span, send_sem, recv_sem):
+        for sem in (recv_sem, send_sem):
+            pltpu.make_async_copy(span, span, sem).wait()
+
     barrier = pltpu.get_barrier_semaphore()
 
     near = max(sizes) // 2 <= ROUNDS
@@ -235,7 +253,7 @@
     alone = nx == 2
 
     (xs, xr, ys, yr, es, er, yl, zs, zr, hs, hr, ds, dr, cs, cr, work, send_sem, recv_sem) = scratch[:BUFFERS]
-    grown, sent, rims, side, hz, t2r, t3r, o1s, o2s, m_send, m_recv = scratch[BUFFERS : BUFFERS + 11]
+    grown, sent, side, hz, t2r, t3r, o1s, o2s, m_send, m_recv = scratch[BUFFERS : BUFFERS + 10]
     s = 1
     n = field.shape[2] // s
     px = field.shape[1] // s
@@ -288,17 +306,8 @@
         copies.append((xs.at[a], xr.at[a], (away[a], 0, 0)))
     for i in (0, 1):
         copies.append((zs, zr.at[i], (0, 0, away[i])))
-    flights = [
-        pltpu.make_async_remote_copy(
-            src_ref=f, dst_ref=t, send_sem=send_sem.at[i], recv_sem=recv_sem.at[i],
-            device_id=device(*d), device_id_type=MESH,
-        )
-        for i, (f, t, d) in enumerate(copies)
-    ]
-    for flight in flights:
-        flight.start()
-    for flight in flights:
-        flight.wait()
+    sent_rows = launch(copies, send_sem, recv_sem)
+    settle(grown.at[pl.ds(0, sent_rows)], send_sem, recv_sem)
 
     for b in (0, 1):
         yl[b] = lift_rows(yr[b], er[2 + b], er[b])
@@ -400,18 +409,9 @@
         rows_copy(px_rows // 2 * gx, px_rows // parts, (step_to[gx], 0, 0))
     for gy in (0, 1):
         rows_copy(px_rows + py_rows // 2 * gy, py_rows // 2, (0, step_to[gy], 0))
-    flights = [
-        pltpu.make_async_remote_copy(
-            src_ref=f, dst_ref=t, send_sem=m_send.at[i], recv_sem=m_recv.at[i],
-            device_id=device(*d), device_id_type=MESH,
-        )
-        for i, (f, t, d) in enumerate(copies)
-    ]
-    for flight in flights:
-        flight.start()
+    sent_rows = launch(copies, m_send, m_recv)
     sums = finish()
-    for flight in flights:
-        flight.wait()
+    settle(grown.at[pl.ds(0, sent_rows)], m_send, m_recv)
 
     lane2 = iota((2, LANES), 1)
     for g in (0, 1):
@@ -471,11 +471,12 @@
     for i, whole in enumerate(sums):
         tail = jnp.where(one == i, whole, tail)
     msg[groups:] = jnp.broadcast_to(tail, (msg.shape[0] - groups, LANES))
-    flat = (me[0] * ny + me[1]) * nz + me[2]
+
+    slot = (me[2] * nx + me[0]) * ny + me[1]
 
     def post(j):
         return pltpu.make_async_remote_copy(
-            src_ref=msg, dst_ref=gath.at[flat], send_sem=g_send.at[j], recv_sem=g_recv.at[j],
+            src_ref=msg, dst_ref=gath.at[slot], send_sem=g_send, recv_sem=g_recv,
             device_id=device(*split(j)), device_id_type=MESH,
         )
 
@@ -483,45 +484,27 @@
         post(ndev - j).start()
         return carry
 
-    def settle(j, carry):
-        post(j).wait()
-        return carry
-
-    def place_all():
-        place(lambda x: o1s[pl.ds(x * ay, ay), :], 1)
-        place(lambda x: o2s[x], 2)
-
     if ndev <= 32:
-        posts = [post(ndev - j) for j in range(1, ndev)]
-        for flight in posts:
-            flight.start()
-        gath[flat] = msg[...]
-        place_all()
-        for flight in posts:
-            flight.wait()
+        for j in range(1, ndev):
+            post(ndev - j).start()
     else:
         lax.fori_loop(1, ndev, send, 0)
-        gath[flat] = msg[...]
-        place_all()
-        lax.fori_loop(1, ndev, settle, 0)
-
-    sub = iota((8, LANES), 0)
-    lane8 = iota((8, LANES), 1)
-
-    def unpack(d, tail):
-        for g in range(groups):
-            acc = jnp.zeros((8, LANES), jnp.float32)
+    gath[slot] = msg[...]
+    place(lambda x: o1s[pl.ds(x * ay, ay), :], 1)
+    place(lambda x: o2s[x], 2)
+    settle(gath.at[pl.ds(0, ndev - 1)], g_send, g_recv)
+
+    spots = nx * ny
+    at = iota((spots, LANES), 1) % step
+    tail = jnp.zeros((1, LANES), jnp.float32)
+    for g in range(groups):
+        boxes = [gath[pl.ds(z * spots, spots), g, :] for z in range(nz)]
+        for bit in range(8):
+            v = jnp.zeros((spots, LANES), jnp.float32)
             for z in range(nz):
-                v = jnp.broadcast_to(gath[d * nz + z, g : g + 1, :], (8, LANES))
-                for bit in (1, 2, 4):
-                    v = jnp.where((sub & bit) != 0, roll(v, -bit, 1), v)
-                acc += roll(jnp.where(lane8 % step == 0, v, 0.0), z, 1)
-            final_s[pl.ds(pl.multiple_of(d * count + 8 * g, 8), 8), :] = acc
-        for z in range(nz):
-            tail += gath[d * nz + z, groups : groups + 1, :]
-        return tail
-
-    tail = lax.fori_loop(0, nx * ny, unpack, jnp.zeros((1, LANES), jnp.float32), unroll=nx * ny <= 8)
+                v = jnp.where(at == z, roll(boxes[z], z - bit, 1), v)
+            final_s[pl.ds((bit * groups + g) * spots, spots), :] = v
+    tail = jnp.sum(gath[:, groups, :], axis=0, keepdims=True)
 
     def dot(a, b):
         return jnp.dot(a, b, precision=lax.Precision.HIGHEST, preferred_element_type=jnp.float32)
@@ -598,14 +581,14 @@
             (2, lx, LANES), (ly, LANES), (2, ly, LANES), (ly, LANES), (4, ly, LANES), (2, 1, LANES),
             (4, 1, LANES), (2, 1, LANES), (8, 1, LANES), (lx, ly, LANES),
         )),
-        pltpu.SemaphoreType.DMA((26,)),
-        pltpu.SemaphoreType.DMA((26,)),
+        pltpu.SemaphoreType.DMA,
+        pltpu.SemaphoreType.DMA,
         *(pltpu.VMEM(shape, jnp.float32) for shape in (
-            (own + extra, LANES), (extra, LANES), (1, LANES), (2, 2, own + 2 * LANES), (2, 2, own + 2 * LANES),
+            (own + extra, LANES), (extra, LANES), (2, 2, own + 2 * LANES), (2, 2, own + 2 * LANES),
             (2, 4, 2, LANES), (2, 2, 2, 2, LANES), (own, LANES), (lx // 4, ly // 4, LANES),
         )),
-        pltpu.SemaphoreType.DMA((26,)),
-        pltpu.SemaphoreType.DMA((26,)),
+        pltpu.SemaphoreType.DMA,
+        pltpu.SemaphoreType.DMA,
     ]
     height = -(-(count // 8 + 1) // 4) * 4
     scratch += [
@@ -613,8 +596,8 @@
         pltpu.VMEM((height, LANES), jnp.float32),
         pltpu.VMEM((count, LANES), jnp.float32),
         pltpu.VMEM((nx * ny * count, LANES), jnp.float32),
-        pltpu.SemaphoreType.DMA((ndev,)),
-        pltpu.SemaphoreType.DMA((ndev,)),
+        pltpu.SemaphoreType.DMA,
+        pltpu.SemaphoreType.DMA,
         pltpu.VMEM(fields.shape, jnp.float32),
         pltpu.SMEM(exponents.shape, jnp.int32),
         pltpu.VMEM(tables[0].shape, jnp.float32),

time: 27.6 us -> 25.3 us (0.917)
  Pallas kernels: 26.8 us -> 24.5 us
    pallas_call x1, Pallas kernels: 26 us -> 23.6 us  [shards(): pl.pallas_call(functools.partial(kernel, sizes, cells), out_shape=(pltpu....]
where the time goes in v3:
time: 25.3 us; the launch traced here: 25.1 us
  Pallas kernels  24.5 us (97%)
  between operations  0.64 us (3%)
    pallas_call x1, Pallas kernels, shards(): pl.pallas_call(functools.partial(kernel, sizes, cells), out_shape=(pltpu....  23.6 us
    pallas_call x1, Pallas kernels, shards(): pl.pallas_call(deliver, out_shape=(jax.ShapeDtypeStruct(fields.shape, jnp...  0.83 us

profile of v3, /device:TPU:0, one launch (start us, length us, event | category | flops | bytes accessed | tf_op | source)
XLA Modules:
  0.0 25.1 jit_solution(15608572259060740877)
XLA Ops:
  0.6 23.6 %shard_map.122 = (f32[1,32,32,128]{3,2,1,0:T(8,128)S(1)}, f32[2,1,5]{2,1,0:T(1,128)S(1)}) custom-call(s32[5]{0:T(128)} %exps_in.1, f32[1,32,32,128]{3,2,1,0:T(8,128)} %field_in.1, f32[2,128,128]{2,1,0:T(8,128)} %constant.18.clone.rows_in, f32[2,128,128]{2,1,0:T(8,128)} %constant.19.clone.lanes_in, bf16[144,256]{1,0:T(8,128)(2,1)} %constant.20.clone.rest_0_, ...), custom_call_target="tpu_custom_call" | custom-call | tf_op jit(solution)/shard_map/pallas_call | solution.py:609
  24.3 0.8 %shard_map.123 = (f32[1,32,32,128]{3,2,1,0:T(8,128)}, f32[2,1,5]{2,1,0:T(1,128)}) custom-call(f32[1,32,32,128]{3,2,1,0:T(8,128)S(1)} %get-tuple-element.4.held, f32[2,1,5]{2,1,0:T(1,128)S(1)} %get-tuple-element.5.held_stats), custom_call_target="tpu_custom_call" | custom-call | tf_op jit(solution)/shard_map/pallas_call | solution.py:623

commit v4 on v3

--- a/solution.py
+++ b/solution.py
@@ -14,7 +14,8 @@
 LANES = 128
 CHUNKS = 4
 BUFFERS = 18
-TABLES = 7
+TABLES = 10
+BATCH = 8
 ROUNDS = 2
 VMEM_LIMIT = 33_554_432
 MESH = pl.DeviceIdType.MESH
@@ -87,6 +88,21 @@
     return sent, first, lift_line(n // 2)
 
 
+def fine_tables(px):
+    q = LANES // px
+    ends = np.zeros((2, px))
+    ends[0, px - 1], ends[0, px - 2], ends[1, 0] = 1.0, -0.5, 1.0
+    edges = np.zeros((8, LANES))
+    place = np.zeros((16, LANES))
+    for z in range(2):
+        for x in range(2):
+            edges[2 * z + x, 1 + z :: q] = ends[x]
+            for part in range(3):
+                place[4 * part + 2 * z + x, (LANES - q) * x + 1 + z] = 1.0
+    result = (lift_line(LANES)[:, :LANES].T, edges, place)
+    return tuple(table.astype(jnp.bfloat16) for table in result)
+
+
 def middle_tables(ax, ay, az):
     step = LANES // az
     sent_x, first_x, second_x = line_tables(ax)
@@ -156,12 +172,13 @@
     return jnp.where(odd, w, w + 0.25 * (down + roll(w, -1, 0)))
 
 
-def lift_lanes(v, rim, s):
+def lift_groups(v, rim, s):
     lane = iota(v.shape, 1)
-    up = jnp.where(lane == LANES - s, rim, roll(v, -s, 1))
-    w = jnp.where(lane % (2 * s) == s, v - 0.5 * (roll(v, s, 1) + up), v)
-    down = jnp.where(lane == 0, rim - 0.5 * v, roll(w, s, 1))
-    return jnp.where(lane % (2 * s) == 0, w + 0.25 * (down + roll(w, -s, 1)), w)
+    odd = (lane // s) % 2 == 1
+    up = jnp.where(lane >= LANES - s, rim, roll(v, -s, 1))
+    w = jnp.where(odd, v - 0.5 * (roll(v, s, 1) + up), v)
+    down = jnp.where(lane < s, rim - 0.5 * v, roll(w, s, 1))
+    return jnp.where(odd, w, w + 0.25 * (down + roll(w, -s, 1)))
 
 
 def shrink(v, thresh):
@@ -249,97 +266,129 @@
     gath, msg, rows_s, final_s, g_send, g_recv = scratch[-6:]
     loads[0].wait()
     loads[1].wait()
-    away = (-1, 1)
+    step_to = (1, -1)
     alone = nx == 2
-
-    (xs, xr, ys, yr, es, er, yl, zs, zr, hs, hr, ds, dr, cs, cr, work, send_sem, recv_sem) = scratch[:BUFFERS]
+    ways = (0,) if alone else (0, 1)
+    (xs, xr, ys, yr, es, er, yl, zs, zr, ds, dr, ts, txr, tcr, rim, work, send_sem, recv_sem) = scratch[:BUFFERS]
     grown, sent, side, hz, t2r, t3r, o1s, o2s, m_send, m_recv = scratch[BUFFERS : BUFFERS + 10]
-    s = 1
-    n = field.shape[2] // s
-    px = field.shape[1] // s
+    fine_lanes, fine_edges, fine_place, *tables = tables
     src = field.at[0]
+    px, n = src.shape[0], src.shape[1]
+    half, q = n // 2, LANES // px
     lane = iota((n, LANES), 1)
-
-    def edge(v):
-        return v[0:1], v[n - 1 : n] - 0.5 * v[n - 2 : n - 1]
-
-    e_plane = src[0]
-    p_plane = src[px - 1] - 0.5 * src[px - 2]
-    xs[0] = e_plane
-    xs[1] = p_plane
-    ys[0] = src[:, 0, :]
-    ys[1] = src[:, n - 1, :] - 0.5 * src[:, n - 2, :]
-    for a, plane in ((0, e_plane), (1, p_plane)):
-        es[2 * a], es[2 * a + 1] = edge(plane)
-
+    row8 = iota((8, LANES), 0)
+
+    def ends(v):
+        return v[n - 1 : n] - 0.5 * v[n - 2 : n - 1], v[0:1]
+
+    def under(pair):
+        return jnp.where(row8 == 0, pair[0], jnp.where(row8 == 1, pair[1], 0.0))
+
+    planes = (src[px - 1] - 0.5 * src[px - 2], src[0])
+    ys[0] = src[:, n - 1, :] - 0.5 * src[:, n - 2, :]
+    ys[1] = src[:, 0, :]
+    for gx in (0, 1):
+        xs[gx] = planes[gx]
+        es[2 * gx], es[2 * gx + 1] = ends(planes[gx])
     packed = jnp.zeros((n, LANES), jnp.float32)
     for x in range(px):
-        v = src[x]
-        u = jnp.where(lane == LANES - s, v - 0.5 * roll(v, s, 1), v)
-        at = 2 * s * x
-        packed = jnp.where((lane == at) | (lane == at + s), roll(u, at + s, 1), packed)
-    half = 2 * s * px
-    combined = packed - 0.5 * roll(packed, 2 * s, 1)
-    sides = roll(jnp.where(lane < half // 2, packed, combined), half, 1)
+        packed = jnp.where(lane // q == x, roll(src[x], q * x + 2, 1), packed)
+    packed = jnp.where(lane % q == 1, packed - 0.5 * roll(packed, 1, 1), packed)
     zs[...] = packed
-    hs[...] = sides
-    ds[0], ds[1] = edge(packed)
-    cs[0], cs[1] = edge(sides)
+    ds[0], ds[1] = ends(packed)
+    for load in loads[2:5]:
+        load.wait()
+    edges = sum(
+        mix(fine_edges[...], part, ((1,), (1,)))
+        for part in three(jnp.concatenate((packed, under(ends(packed))), axis=0))
+    )
+    ts[...] = jnp.zeros(ts.shape, jnp.float32)
+    for g in (0, 1):
+        ts[g, :, pl.ds(0, n + 8)] = edges[2 * g : 2 * g + 2]
 
     pl.semaphore_wait(barrier, len(greeted))
     copies = []
-    ways = (0,) if alone else (0, 1)
-    for i in (0, 1):
-        for b in (0, 1):
-            for a in ways:
-                copies.append((cs.at[b], cr.at[4 * a + 2 * b + i], (away[a], away[b], away[i])))
-            copies.append((ds.at[b], dr.at[2 * b + i], (0, away[b], away[i])))
-    for a in (0, 1):
-        for b in (0, 1):
-            copies.append((es.at[2 * a + b], er.at[2 * a + b], (away[a], away[b], 0)))
-    for b in (0, 1):
-        copies.append((ys.at[b], yr.at[b], (0, away[b], 0)))
-    for i in (0, 1):
-        for a in ways:
-            copies.append((hs, hr.at[2 * a + i], (away[a], 0, away[i])))
-    for a in (0, 1):
-        copies.append((xs.at[a], xr.at[a], (away[a], 0, 0)))
-    for i in (0, 1):
-        copies.append((zs, zr.at[i], (0, 0, away[i])))
+    for g in (0, 1):
+        dz = step_to[g]
+        for gx in ways:
+            for gy in (0, 1):
+                copies.append((ts.at[g], tcr.at[g, gy, gx], (step_to[gx], step_to[gy], dz)))
+            copies.append((ts.at[g], txr.at[g, gx], (step_to[gx], 0, dz)))
+        for gy in (0, 1):
+            copies.append((ds.at[gy], dr.at[2 * g + gy], (0, step_to[gy], dz)))
+    for gx in (0, 1):
+        for gy in (0, 1):
+            copies.append((es.at[2 * gx + gy], er.at[2 * gx + gy], (step_to[gx], step_to[gy], 0)))
+    for g in (0, 1):
+        copies.append((xs.at[g], xr.at[g], (step_to[g], 0, 0)))
+    for g in (0, 1):
+        copies.append((ys.at[g], yr.at[g], (0, step_to[g], 0)))
+    for g in (0, 1):
+        copies.append((zs, zr.at[g], (0, 0, step_to[g])))
     sent_rows = launch(copies, send_sem, recv_sem)
     settle(grown.at[pl.ds(0, sent_rows)], send_sem, recv_sem)
 
-    for b in (0, 1):
-        yl[b] = lift_rows(yr[b], er[2 + b], er[b])
-
-    def rim_of(main, side):
-        spot = iota(main(0).shape, 1)
-        parts = []
-        for i in (0, 1):
-            after = side(0, i)
-            before = after if alone else side(1, i)
-            v = jnp.where(spot < half, main(i), 0.0)
-            v = jnp.where((spot >= half) & (spot < half + 2 * s), after, v)
-            parts.append(jnp.where(spot >= LANES - 2 * s, before, v))
-        v = jnp.where(spot % (2 * s) < s, roll(parts[0], -s, 1), roll(parts[1], s, 1))
-        odd = (spot // (2 * s)) % 2 == 1
-        w = jnp.where(odd, v - 0.5 * (roll(v, 2 * s, 1) + roll(v, -2 * s, 1)), v)
-        return jnp.where(odd, w, w + 0.25 * (roll(w, 2 * s, 1) + roll(w, -2 * s, 1)))
-
-    rim_rows = [
-        rim_of(lambda i: dr[2 * b + i], lambda a, i: cr[4 * a + 2 * b + i]) for b in (0, 1)
-    ]
-    rim = rim_of(lambda i: zr[i], lambda a, i: hr[2 * a + i])
-    rim = lift_rows(rim, rim_rows[1], rim_rows[0])
+    lane2, row2 = iota((2, LANES), 1), iota((2, LANES), 0)
+    for g in (0, 1):
+        yl[g] = lift_rows(yr[g], er[g], er[2 + g])
+
+    def both(ref):
+        return ref[0] if alone else jnp.where(row2 == 0, ref[0], ref[1])
+
+    def columns(top, table):
+        pieces = [part.astype(jnp.float32) for part in three(top)]
+        pieces.append(jnp.zeros_like(top))
+        return mix(jnp.concatenate(pieces, axis=0).astype(jnp.bfloat16), table, ((0,), (0,)))
+
+    tops = []
+    for g in (0, 1):
+        v = jnp.where(lane2 == n, both(tcr.at[g, 0]), both(tcr.at[g, 1]))
+        v = jnp.where(lane2 < n, both(txr.at[g]), v)
+        tops.append(jnp.where(lane2 < n + 2, v, 0.0))
+    beside = columns(jnp.concatenate(tops, axis=0), fine_place[...])[0 : n + 8]
+
+    def kinds(a, b):
+        return jnp.where(iota(a.shape, 1) % q == 1, a, b)
+
+    lower = under((kinds(dr[0], dr[2]), kinds(dr[1], dr[3])))
+    v = lift_groups(jnp.concatenate((kinds(zr[0], zr[1]), lower), axis=0), beside, q)
+    v = lift_rows(v[0:n], v[n : n + 1], v[n + 1 : n + 2])
+    v = jnp.where(lane % q == 2, roll(v, 1, 1), jnp.where(lane % q == 1, roll(v, -1, 1), roll(v, -2, 1)))
+    rim[...] = v
+    border = jnp.concatenate((rim[pl.ds(0, half, stride=2), :], rim[pl.ds(1, half, stride=2), :]), axis=0)
+    share = jnp.where(lane == LANES - 1, -0.5, jnp.where(lane == LANES - 2, -0.125, jnp.where(lane == 0, 0.25, 0.0)))
     level_thresh = thresh(0)
-    inner = (lane % (2 * s) == 0) & (iota((n, LANES), 0) % 2 == 0)
-
-    def plane_step(x, v):
-        v = lift_rows(v, yl[1, x : x + 1, :], yl[0, x : x + 1, :])
-        v = lift_lanes(v, roll(rim, LANES - s - 2 * s * x, 1), s)
-        work[x] = v
-        if x % 2 == 0:
-            grown[pl.ds(x // 2 * (n // 2), n // 2), :] = work[x, pl.ds(0, n // 2, stride=2), :]
+    inner = (iota((n, LANES), 0) < half) & (lane % 2 == 0)
+    row = iota((half, LANES), 0)
+
+    def halves(ref, x):
+        return [ref[x, pl.ds(start, half, stride=2), :] for start in (0, 1)]
+
+    def lift_halves(v, x):
+        even, odd = v
+        after = jnp.where(row == half - 1, yl[1, x : x + 1, :], roll(even, -1, 0))
+        detail = odd - 0.5 * (even + after)
+        before = jnp.where(row == 0, yl[0, x : x + 1, :] - 0.5 * even, roll(detail, 1, 0))
+        return [even + 0.25 * (before + detail), detail]
+
+    even = halves(src, 0)
+    before = [p - 0.5 * e for p, e in zip(halves(xr, 0), even)]
+    stack = []
+    for k in range(px // 2):
+        after = halves(src, 2 * k + 2) if 2 * k + 2 < px else halves(xr, 1)
+        detail = [o - 0.5 * (e + a) for o, e, a in zip(halves(src, 2 * k + 1), even, after)]
+        smooth = [e + 0.25 * (b + d) for e, b, d in zip(even, before, detail)]
+        stack += lift_halves(smooth, 2 * k) + lift_halves(detail, 2 * k + 1)
+        even, before = after, detail
+        if len(stack) == 2 * BATCH:
+            wide = mix_lanes(jnp.concatenate(stack, axis=0), fine_lanes[...])
+            for i in range(BATCH):
+                x = 2 * k + 2 - BATCH + i
+                v = wide[n * i : n * i + n] + roll(border, LANES - 2 - q * x, 1) * share
+                work[x] = v
+                if x % 2 == 0:
+                    grown[pl.ds(x // 2 * half, half), :] = v[0:half]
+            stack = []
 
     def finish():
         energy = kept = jnp.zeros((n, LANES), jnp.float32)
@@ -352,23 +401,14 @@
             else:
                 energy += v * v
                 kept += jnp.abs(small)
-            out[0, x] = small
+            for start in (0, 1):
+                out[0, x, pl.ds(start, half, stride=2), :] = small[half * start : half * start + half]
         return [total(energy), total(kept)]
-
-    even = src[0]
-    before = xr[1] - 0.5 * even
-    for k in range(px // 2):
-        after = src[2 * k + 2] if 2 * k + 2 < px else xr[0]
-        detail = src[2 * k + 1] - 0.5 * (even + after)
-        smooth = even + 0.25 * (before + detail)
-        plane_step(2 * k, smooth)
-        plane_step(2 * k + 1, detail)
-        even, before = after, detail
 
     ax, ay = px // 2, n // 2
     own = ax * ay
     send_rows, rows1, rows2, send_lanes, lanes1, rim1, lanes2 = tables
-    for load in loads[2 : 2 + TABLES]:
+    for load in loads[5 : 2 + TABLES]:
         load.wait()
     here = grown[0:own]
     halo = mix_rows(send_rows[...], here)
@@ -382,7 +422,6 @@
         side[g, :, pl.ds(own, 2 * LANES)] = jnp.zeros((2, 2 * LANES), jnp.float32)
         side[g, :, pl.ds(0, own + extra)] = edges[2 * g : 2 * g + 2]
 
-    step_to = (1, -1)
     px_rows, py_rows = 4 * ay, 4 * ax
     copies = []
     for g in (0, 1):
@@ -413,7 +452,6 @@
     sums = finish()
     settle(grown.at[pl.ds(0, sent_rows)], m_send, m_recv)
 
-    lane2 = iota((2, LANES), 1)
     for g in (0, 1):
         v = jnp.where(lane2 < px_rows // 2, t2r[g, 0], t2r[g, 0 if alone else 1])
         v = jnp.where(lane2 < px_rows, v, jnp.where(lane2 < px_rows + py_rows // 2, t2r[g, 2], t2r[g, 3]))
@@ -423,11 +461,7 @@
             u.append(jnp.where(lane2 % 8 < 4, t3r[g, gy, 0], t3r[g, gy, 0 if alone else 1]))
         v = jnp.where(lane2 < 8, u[0], u[1])
         hz[g, :, pl.ds(own + LANES, LANES)] = jnp.where(lane2 < 16, v, 0.0)
-    pieces = []
-    for part in three(jnp.concatenate((hz[0], hz[1]), axis=0)):
-        pieces.append(part.astype(jnp.float32))
-    pieces.append(jnp.zeros_like(pieces[0]))
-    rim_rows = mix(jnp.concatenate(pieces, axis=0).astype(jnp.bfloat16), rim1[...], ((0,), (0,)))
+    rim_rows = columns(jnp.concatenate((hz[0], hz[1]), axis=0), rim1[...])
     wide = mix_lanes(grown[...], lanes1[...]) + rim_rows[0 : own + extra]
     first = mix_rows(rows1[...], wide)
     second = mix_lanes(mix_rows(rows2[...], first), lanes2[...])
@@ -575,11 +609,12 @@
     tables = coarse_matrices(sizes, coarse)
     middle = middle_tables(lx // 2, ly // 2, lz // 2)
     own, extra = lx // 2 * (ly // 2), middle[0].shape[0]
+    middle = fine_tables(lx) + middle
     scratch = [
         *(pltpu.VMEM(shape, jnp.float32) for shape in (
             (2, ly, LANES), (2, ly, LANES), (2, lx, LANES), (2, lx, LANES), (4, 1, LANES), (4, 1, LANES),
-            (2, lx, LANES), (ly, LANES), (2, ly, LANES), (ly, LANES), (4, ly, LANES), (2, 1, LANES),
-            (4, 1, LANES), (2, 1, LANES), (8, 1, LANES), (lx, ly, LANES),
+            (2, lx, LANES), (ly, LANES), (2, ly, LANES), (2, 1, LANES), (4, 1, LANES), (2, 2, LANES),
+            (2, 2, 2, LANES), (2, 2, 2, 2, LANES), (ly, LANES), (lx, ly, LANES),
         )),
         pltpu.SemaphoreType.DMA,
         pltpu.SemaphoreType.DMA,

time: 25.3 us -> 23.2 us (0.917)
  Pallas kernels: 24.5 us -> 22.4 us
    pallas_call x1, Pallas kernels: 23.6 us -> 21.6 us  [shards(): pl.pallas_call(functools.partial(kernel, sizes, cells), out_shape=(pltpu....]
where the time goes in v4:
time: 23.2 us; the launch traced here: 23.1 us
  Pallas kernels  22.4 us (97%)
  between operations  0.64 us (3%)
    pallas_call x1, Pallas kernels, shards(): pl.pallas_call(functools.partial(kernel, sizes, cells), out_shape=(pltpu....  21.6 us
    pallas_call x1, Pallas kernels, shards(): pl.pallas_call(deliver, out_shape=(jax.ShapeDtypeStruct(fields.shape, jnp...  0.83 us

profile of v4, /device:TPU:0, one launch (start us, length us, event | category | flops | bytes accessed | tf_op | source)
XLA Modules:
  0.0 23.1 jit_solution(15753672629611938620)
XLA Ops:
  0.6 21.6 %shard_map.149 = (f32[1,32,32,128]{3,2,1,0:T(8,128)S(1)}, f32[2,1,5]{2,1,0:T(1,128)S(1)}) custom-call(s32[5]{0:T(128)} %exps_in.1, f32[1,32,32,128]{3,2,1,0:T(8,128)} %field_in.1, f32[2,128,128]{2,1,0:T(8,128)} %constant.24.clone.rows_in, f32[2,128,128]{2,1,0:T(8,128)} %constant.25.clone.lanes_in, bf16[128,128]{1,0:T(8,128)(2,1)} %constant.26.clone.rest_0_, ...), custom_call_target="tpu_custom_call" | custom-call | tf_op jit(solution)/shard_map/pallas_call | solution.py:644
  22.2 0.8 %shard_map.150 = (f32[1,32,32,128]{3,2,1,0:T(8,128)}, f32[2,1,5]{2,1,0:T(1,128)}) custom-call(f32[1,32,32,128]{3,2,1,0:T(8,128)S(1)} %get-tuple-element.4.held, f32[2,1,5]{2,1,0:T(1,128)S(1)} %get-tuple-element.5.held_stats), custom_call_target="tpu_custom_call" | custom-call | tf_op jit(solution)/shard_map/pallas_call | solution.py:658

commit v5 on v4

--- a/solution.py
+++ b/solution.py
@@ -14,10 +14,10 @@
 LANES = 128
 CHUNKS = 4
 BUFFERS = 18
-TABLES = 10
+TABLES = 12
 BATCH = 8
 ROUNDS = 2
-VMEM_LIMIT = 33_554_432
+VMEM_LIMIT = 58_720_256
 MESH = pl.DeviceIdType.MESH
 
 
@@ -47,17 +47,41 @@
     gy = (dev % ny) * cy + inner % cy
     step = LANES // cz
     lanes = np.array([z * step + d for d in range(nz) for z in range(cz)])
-    order = np.arange(nx * ny * cx * cy).reshape(nx * ny, -1, 8).transpose(2, 1, 0).reshape(-1)
+    reach_y, reach_x, spot = np.indices((cy + 3, cx + 3, nx * ny)).reshape(3, -1)
+    from_x = (spot // ny * cx + reach_x - 1) % (nx * cx)
+    from_y = (spot % ny * cy + reach_y - 1) % (ny * cy)
+    from_z = np.arange(-1, nz * cz + 2) % (nz * cz)
     result = []
     for both_levels in (False, True):
         mx, my, mz = periodic_lift(nx * cx), periodic_lift(ny * cy), periodic_lift(nz * cz)
         if both_levels:
             mx, my, mz = second_lift(nx * cx) @ mx, second_lift(ny * cy) @ my, second_lift(nz * cz) @ mz
-        both = mx[gx[:, None], gx[None]] * my[gy[:, None], gy[None]]
+        both = mx[gx[:, None], from_x[None]] * my[gy[:, None], from_y[None]]
         along = np.zeros((LANES, LANES))
-        along[np.ix_(lanes, lanes)] = mz.T
-        result.append((both[:, order].astype(np.float32), along.astype(np.float32)))
+        along[np.ix_(np.arange(len(from_z)), lanes)] = mz[:, from_z].T
+        result.append((both.astype(np.float32), along.astype(np.float32)))
     return [np.stack(pair) for pair in zip(*result)]
+
+
+def reach_line(n):
+    twice = periodic_lift(3 * n // 2)[0::2] @ periodic_lift(3 * n)[0::2]
+    return twice[n // 4 - 1 : n // 2 + 2, n : 2 * n]
+
+
+def reach_tables(ax, ay, az):
+    part_x, part_y, part_z = reach_line(ax), reach_line(ay), reach_line(az)
+    wide, deep = len(part_z), len(part_y)
+    rows = np.zeros((deep, 8, ax * ay))
+    rows[:, : len(part_x)] = np.einsum("yb,xa->yxab", part_y, part_x).reshape(deep, -1, ax * ay)
+    rows = rows.reshape(8 * deep, -1)
+    high = rows.astype(jnp.bfloat16)
+    low = (rows - high.astype(np.float64)).astype(jnp.bfloat16)
+    along = np.zeros((deep + 1, LANES, LANES))
+    for y in range(deep):
+        fit = min(wide, LANES - wide * y)
+        along[y, :: LANES // az, wide * y : wide * y + fit] = part_z[:fit].T
+    along[deep, :: LANES // az, : wide - fit] = part_z[fit:].T
+    return np.concatenate((high, low)), along.reshape(-1, LANES).astype(jnp.bfloat16)
 
 
 def lift_line(n):
@@ -221,8 +245,6 @@
     scratch = scratch[:-5]
     pairs = [(field_in, field), (exps_in, exps), *zip(tables_in, tables), (rows_in, k_s), (lanes_in, l_s)]
     loads = [pltpu.make_async_copy(a, b, in_sem.at[i]) for i, (a, b) in enumerate(pairs)]
-    for load in loads:
-        load.start()
     me = (lax.axis_index("gx"), lax.axis_index("gy"), lax.axis_index("gz"))
 
     def device(dx, dy, dz):
@@ -231,6 +253,9 @@
             lax.rem(me[1] + (dy + ny), ny),
             lax.rem(me[2] + (dz + nz), nz),
         )
+
+    def distance(spot):
+        return sum(min(d, size - d) for d, size in zip(spot, sizes))
 
     def thresh(level):
         return jnp.exp2(jnp.full((1, LANES), exps[level].astype(jnp.float32)))
@@ -261,9 +286,11 @@
         tuple((d + size - 1) % size if near else d for d, size in zip(spot, sizes))
         for spot in np.ndindex(*(3, 3, 3) if near else sizes)
     } - {(0, 0, 0)}
-    for spot in sorted(greeted):
+    for spot in sorted(greeted, key=lambda spot: (-distance(spot), spot)):
         pl.semaphore_signal(barrier, inc=1, device_id=device(*spot), device_id_type=MESH)
-    gath, msg, rows_s, final_s, g_send, g_recv = scratch[-6:]
+    for load in loads:
+        load.start()
+    gath, msg, parts_s, final_s, tally_s, tallies, g_send, g_recv, t_send, t_recv = scratch[-10:]
     loads[0].wait()
     loads[1].wait()
     step_to = (1, -1)
@@ -271,7 +298,7 @@
     ways = (0,) if alone else (0, 1)
     (xs, xr, ys, yr, es, er, yl, zs, zr, ds, dr, ts, txr, tcr, rim, work, send_sem, recv_sem) = scratch[:BUFFERS]
     grown, sent, side, hz, t2r, t3r, o1s, o2s, m_send, m_recv = scratch[BUFFERS : BUFFERS + 10]
-    fine_lanes, fine_edges, fine_place, *tables = tables
+    fine_lanes, fine_edges, fine_place, reach_rows, reach_lanes, *tables = tables
     src = field.at[0]
     px, n = src.shape[0], src.shape[1]
     half, q = n // 2, LANES // px
@@ -449,6 +476,52 @@
     for gy in (0, 1):
         rows_copy(px_rows + py_rows // 2 * gy, py_rows // 2, (0, step_to[gy], 0))
     sent_rows = launch(copies, m_send, m_recv)
+
+    spots = nx * ny
+    slot = (me[2] * nx + me[0]) * ny + me[1]
+    cx, cy, cz = ax // 4, ay // 4, LANES // 2**FINE
+    step = 2**FINE
+    count = cx * cy
+    long, deep, reach = cx + 3, cy + 3, cz + 3
+    cut = LANES - reach * (deep - 1)
+    rest = reach - cut
+
+    def spread(source, target, send_sem, recv_sem):
+        def post(j):
+            return pltpu.make_async_remote_copy(
+                src_ref=source, dst_ref=target, send_sem=send_sem, recv_sem=recv_sem,
+                device_id=device(*split(j)), device_id_type=MESH,
+            )
+
+        def send(j, carry):
+            post(j).start()
+            return carry
+
+        if ndev <= 32:
+            for j in sorted(range(1, ndev), key=lambda j: (-distance(split(j)), j)):
+                post(j).start()
+        else:
+            lax.fori_loop(1, ndev, send, 0)
+
+    pieces = mix_rows(reach_rows[...], here)
+    pieces = pieces[0 : 8 * deep] + pieces[8 * deep :]
+    blocks = [part.astype(jnp.float32) for part in three(pieces)]
+
+    def stack(first, last):
+        rows = [jnp.concatenate([b[8 * y : 8 * y + 8] for y in range(first, last)], axis=1) for b in blocks]
+        return jnp.concatenate(rows + [jnp.zeros_like(rows[0])], axis=0).astype(jnp.bfloat16)
+
+    def fold(v):
+        return v[0:8] + v[8:16] + v[16:24]
+
+    sheet = fold(mix(stack(0, deep), reach_lanes[pl.ds(0, deep * LANES), :], ((1,), (0,))))
+    loose = fold(mix(stack(deep - 1, deep), reach_lanes[pl.ds(deep * LANES, LANES), :], ((1,), (0,))))
+    spare = loose[0:1]
+    for x in range(1, long):
+        spare += roll(loose[x : x + 1], rest * x, 1)
+    msg[...] = jnp.where(row8 == long, spare, sheet)
+    spread(msg, gath.at[slot], g_send, g_recv)
+    gath[slot] = msg[...]
     sums = finish()
     settle(grown.at[pl.ds(0, sent_rows)], m_send, m_recv)
 
@@ -486,64 +559,37 @@
             spot = (0, s * x, pl.ds(0, small_y, stride=s), slice(None))
             out[spot] = jnp.where(keep, shrink(source(x), thresh(level)), out[spot])
 
-    cx, cy = ax // 4, ay // 4
-    step = 2**FINE
-    count = cx * cy
-    for x in range(cx):
-        rows_s[pl.ds(x * cy, cy), :] = o2s[2 * x, pl.ds(0, cy, stride=2), :]
-    here = rows_s[...]
-    lane = iota((count, LANES), 1)
-    row = iota((count, LANES), 0)
-    here = jnp.where(lane % step == 0, here, 0.0)
-    for bit in (1, 2, 4):
-        here = jnp.where((row & bit) != 0, roll(here, bit, 1), here)
-    groups = count // 8
     one = iota((1, LANES), 1)
-    for g in range(groups):
-        msg[g : g + 1] = jnp.sum(here[8 * g : 8 * g + 8], axis=0, keepdims=True)
     tail = jnp.zeros((1, LANES), jnp.float32)
     for i, whole in enumerate(sums):
         tail = jnp.where(one == i, whole, tail)
-    msg[groups:] = jnp.broadcast_to(tail, (msg.shape[0] - groups, LANES))
-
-    slot = (me[2] * nx + me[0]) * ny + me[1]
-
-    def post(j):
-        return pltpu.make_async_remote_copy(
-            src_ref=msg, dst_ref=gath.at[slot], send_sem=g_send, recv_sem=g_recv,
-            device_id=device(*split(j)), device_id_type=MESH,
-        )
-
-    def send(j, carry):
-        post(ndev - j).start()
-        return carry
-
-    if ndev <= 32:
-        for j in range(1, ndev):
-            post(ndev - j).start()
-    else:
-        lax.fori_loop(1, ndev, send, 0)
-    gath[slot] = msg[...]
+    tally_s[...] = tail
+    spread(tally_s, tallies.at[slot], t_send, t_recv)
+    tallies[slot] = tail
     place(lambda x: o1s[pl.ds(x * ay, ay), :], 1)
     place(lambda x: o2s[x], 2)
     settle(gath.at[pl.ds(0, ndev - 1)], g_send, g_recv)
 
-    spots = nx * ny
-    at = iota((spots, LANES), 1) % step
-    tail = jnp.zeros((1, LANES), jnp.float32)
-    for g in range(groups):
-        boxes = [gath[pl.ds(z * spots, spots), g, :] for z in range(nz)]
-        for bit in range(8):
-            v = jnp.zeros((spots, LANES), jnp.float32)
-            for z in range(nz):
-                v = jnp.where(at == z, roll(boxes[z], z - bit, 1), v)
-            final_s[pl.ds((bit * groups + g) * spots, spots), :] = v
-    tail = jnp.sum(gath[:, groups, :], axis=0, keepdims=True)
+    at = iota((spots, LANES), 1)
+    spares = [gath[pl.ds(z * spots, spots), long, :] for z in range(nz)]
+
+    def window(v, source, start, size):
+        moved = roll(v, start - source, 1)
+        return jnp.where((at >= start) & (at < start + size), moved, 0.0)
+
+    for x in range(long):
+        boxes = [gath[pl.ds(z * spots, spots), x, :] for z in range(nz)]
+        for y in range(deep):
+            fit = reach if y < deep - 1 else cut
+            v = sum(window(boxes[z], reach * y, cz * z, fit) for z in range(nz))
+            if fit < reach:
+                v += sum(window(spares[z], rest * x, cz * z + cut, rest) for z in range(nz))
+            parts_s[pl.ds((y * long + x) * spots, spots), :] = v
 
     def dot(a, b):
         return jnp.dot(a, b, precision=lax.Precision.HIGHEST, preferred_element_type=jnp.float32)
 
-    grid = final_s[...]
+    grid = parts_s[...]
     loads[2 + TABLES].wait()
     loads[3 + TABLES].wait()
     half3, half4 = dot(k_s[0], grid), dot(k_s[1], grid)
@@ -566,6 +612,15 @@
 
     coarse = ((masked(det3, grid * grid), masked(det3, jnp.abs(small3))),
               (masked(det4, grid4 * grid4), masked(det4, jnp.abs(small4))))
+    first = pl.multiple_of((me[0] * ny + me[1]) * count, count)
+    mine = pltpu.roll(final_s[pl.ds(first, count), :], lax.rem(LANES - me[2], LANES), 1)
+    keep = iota((cy, LANES), 1) % step == 0
+    for x in range(cx):
+        spot = (0, step * x, pl.ds(0, cy, stride=step), slice(None))
+        out[spot] = jnp.where(keep, mine[x * cy : x * cy + cy], out[spot])
+
+    settle(tallies.at[pl.ds(0, ndev - 1)], t_send, t_recv)
+    tail = jnp.sum(tallies[...], axis=0)
     for q in (0, 1):
         line = jnp.zeros((1, LANES), jnp.float32)
         for level in range(LEVELS):
@@ -576,14 +631,6 @@
                 value = coarse[level - FINE][q]
             line = jnp.where(one == level, value * weight, line)
         stats[q] = line[:, 0:LEVELS]
-
-    first = pl.multiple_of((me[0] * ny + me[1]) * count, count)
-    mine = pltpu.roll(final_s[pl.ds(first, count), :], lax.rem(LANES - me[2], LANES), 1)
-    rows_s[...] = mine
-    keep = iota((cy, LANES), 1) % step == 0
-    for x in range(cx):
-        spot = (0, step * x, pl.ds(0, cy, stride=step), slice(None))
-        out[spot] = jnp.where(keep, rows_s[pl.ds(x * cy, cy), :], out[spot])
 
 
 def deliver(held, held_stats, out, stats, sem):
@@ -609,7 +656,7 @@
     tables = coarse_matrices(sizes, coarse)
     middle = middle_tables(lx // 2, ly // 2, lz // 2)
     own, extra = lx // 2 * (ly // 2), middle[0].shape[0]
-    middle = fine_tables(lx) + middle
+    middle = fine_tables(lx) + reach_tables(lx // 2, ly // 2, lz // 2) + middle
     scratch = [
         *(pltpu.VMEM(shape, jnp.float32) for shape in (
             (2, ly, LANES), (2, ly, LANES), (2, lx, LANES), (2, lx, LANES), (4, 1, LANES), (4, 1, LANES),
@@ -625,14 +672,14 @@
         pltpu.SemaphoreType.DMA,
         pltpu.SemaphoreType.DMA,
     ]
-    height = -(-(count // 8 + 1) // 4) * 4
     scratch += [
-        pltpu.VMEM((ndev, height, LANES), jnp.float32),
-        pltpu.VMEM((height, LANES), jnp.float32),
-        pltpu.VMEM((count, LANES), jnp.float32),
+        pltpu.VMEM((ndev, 8, LANES), jnp.float32),
+        pltpu.VMEM((8, LANES), jnp.float32),
+        pltpu.VMEM((tables[0].shape[2], LANES), jnp.float32),
         pltpu.VMEM((nx * ny * count, LANES), jnp.float32),
-        pltpu.SemaphoreType.DMA,
-        pltpu.SemaphoreType.DMA,
+        pltpu.VMEM((1, LANES), jnp.float32),
+        pltpu.VMEM((ndev, 1, LANES), jnp.float32),
+        *[pltpu.SemaphoreType.DMA] * 4,
         pltpu.VMEM(fields.shape, jnp.float32),
         pltpu.SMEM(exponents.shape, jnp.int32),
         pltpu.VMEM(tables[0].shape, jnp.float32),

time: 23.2 us -> 22.5 us (0.970)
  Pallas kernels: 22.4 us -> 21.7 us
    pallas_call x1, Pallas kernels: 21.6 us -> 20.9 us  [shards(): pl.pallas_call(functools.partial(kernel, sizes, cells), out_shape=(pltpu....]
where the time goes in v5:
time: 22.5 us; the launch traced here: 22.3 us
  Pallas kernels  21.7 us (96%)
  between operations  0.64 us (3%)
    pallas_call x1, Pallas kernels, shards(): pl.pallas_call(functools.partial(kernel, sizes, cells), out_shape=(pltpu....  20.9 us
    pallas_call x1, Pallas kernels, shards(): pl.pallas_call(deliver, out_shape=(jax.ShapeDtypeStruct(fields.shape, jnp...  0.83 us

profile of v5, /device:TPU:0, one launch (start us, length us, event | category | flops | bytes accessed | tf_op | source)
XLA Modules:
  0.0 22.3 jit_solution(17869826669821477878)
XLA Ops:
  0.6 20.9 %shard_map.167 = (f32[1,32,32,128]{3,2,1,0:T(8,128)S(1)}, f32[2,1,5]{2,1,0:T(1,128)S(1)}) custom-call(s32[5]{0:T(128)} %exps_in.1, f32[1,32,32,128]{3,2,1,0:T(8,128)} %field_in.1, f32[2,128,392]{2,1,0:T(8,128)} %constant.28.clone.rows_in, f32[2,128,128]{2,1,0:T(8,128)} %constant.29.clone.lanes_in, bf16[128,128]{1,0:T(8,128)(2,1)} %constant.30.clone.rest_0_, ...), custom_call_target="tpu_custom_call" | custom-call | tf_op jit(solution)/shard_map/pallas_call | solution.py:691
  21.5 0.8 %shard_map.168 = (f32[1,32,32,128]{3,2,1,0:T(8,128)}, f32[2,1,5]{2,1,0:T(1,128)}) custom-call(f32[1,32,32,128]{3,2,1,0:T(8,128)S(1)} %get-tuple-element.4.held, f32[2,1,5]{2,1,0:T(1,128)S(1)} %get-tuple-element.5.held_stats), custom_call_target="tpu_custom_call" | custom-call | tf_op jit(solution)/shard_map/pallas_call | solution.py:705

commit v6 on v5

--- a/solution.py
+++ b/solution.py
@@ -63,6 +63,12 @@
     return [np.stack(pair) for pair in zip(*result)]
 
 
+def cut_table(table):
+    high = table.astype(jnp.bfloat16)
+    low = (table - high.astype(np.float64)).astype(jnp.bfloat16)
+    return high, low
+
+
 def reach_line(n):
     twice = periodic_lift(3 * n // 2)[0::2] @ periodic_lift(3 * n)[0::2]
     return twice[n // 4 - 1 : n // 2 + 2, n : 2 * n]
@@ -74,14 +80,12 @@
     rows = np.zeros((deep, 8, ax * ay))
     rows[:, : len(part_x)] = np.einsum("yb,xa->yxab", part_y, part_x).reshape(deep, -1, ax * ay)
     rows = rows.reshape(8 * deep, -1)
-    high = rows.astype(jnp.bfloat16)
-    low = (rows - high.astype(np.float64)).astype(jnp.bfloat16)
     along = np.zeros((deep + 1, LANES, LANES))
     for y in range(deep):
         fit = min(wide, LANES - wide * y)
         along[y, :: LANES // az, wide * y : wide * y + fit] = part_z[:fit].T
     along[deep, :: LANES // az, : wide - fit] = part_z[fit:].T
-    return np.concatenate((high, low)), along.reshape(-1, LANES).astype(jnp.bfloat16)
+    return np.concatenate(cut_table(rows)), along.reshape(-1, LANES).astype(jnp.bfloat16)
 
 
 def lift_line(n):
@@ -134,8 +138,10 @@
     sent_z, first_z, second_z = line_tables(az)
     own = [(x, y) for x in range(ax) for y in range(ay)]
     corners = [(x, 2 * g + y) for g in range(2) for x in range(4) for y in range(2)]
-    extra = [(ax + k, y) for k in range(4) for y in range(ay)]
-    extra += [(x, ay + k) for k in range(4) for x in range(ax)]
+    extra = []
+    for start in range(2):
+        extra += [(ax + k, y) for k in (start, start + 2) for y in range(ay)]
+        extra += [(x, ay + k) for k in (start, start + 2) for x in range(ax)]
     extra += [(ax + x, ay + y) for x, y in corners]
     taken = np.array(own + extra)
     given = own + [(ax + k, y) for k in range(2) for y in range(0, ay, 2)]
@@ -174,7 +180,10 @@
     along_last = np.zeros((LANES, LANES))
     source = np.concatenate((lanes[0::2], [1, step + 1]))
     along_last[np.ix_(source, lanes[0::2])] = second_z.T
-    result = (send_rows, rows, last, send_lanes, along, rim, along_last)
+    last = np.concatenate(cut_table(last @ rows))
+    along = np.concatenate((along, along @ along_last), axis=1)
+    rim = np.concatenate((rim, rim @ along_last), axis=1)
+    result = (send_rows, rows[: len(own)], last, send_lanes, along, np.roll(along, 1, 0), rim)
     return tuple(table.astype(jnp.bfloat16) for table in result)
 
 
@@ -224,6 +233,10 @@
 def mix_rows(table, v):
     wide = mix(table, jnp.concatenate(three(v), axis=1), ((1,), (0,)))
     return wide[:, :LANES] + wide[:, LANES : 2 * LANES] + wide[:, 2 * LANES :]
+
+
+def doubled(v, n):
+    return v[0:n] + v[n:]
 
 
 def mix_lanes(v, table):
@@ -434,12 +447,16 @@
 
     ax, ay = px // 2, n // 2
     own = ax * ay
-    send_rows, rows1, rows2, send_lanes, lanes1, rim1, lanes2 = tables
+    send_rows, rows1, rows2, send_lanes, lanes12, odd_lanes12, rim12 = tables
     for load in loads[5 : 2 + TABLES]:
         load.wait()
     here = grown[0:own]
     halo = mix_rows(send_rows[...], here)
-    sent[...] = halo
+    px_rows, py_rows = 2 * ay, 2 * ax
+    pair = px_rows + py_rows
+    second_kind = roll(halo[pair : 2 * pair], 1, 1)
+    sent[0:pair] = jnp.where(iota(second_kind.shape, 1) % 2 == 0, halo[0:pair], second_kind)
+    sent[pair:] = halo[2 * pair :]
     edges = sum(
         mix(send_lanes[...], part, ((1,), (1,)))
         for part in three(jnp.concatenate((here, halo), axis=0))
@@ -449,7 +466,6 @@
         side[g, :, pl.ds(own, 2 * LANES)] = jnp.zeros((2, 2 * LANES), jnp.float32)
         side[g, :, pl.ds(0, own + extra)] = edges[2 * g : 2 * g + 2]
 
-    px_rows, py_rows = 4 * ay, 4 * ax
     copies = []
     for g in (0, 1):
         dz = step_to[g]
@@ -470,7 +486,7 @@
     parts = len(ways)
     for gy in (0, 1):
         for gx in ways:
-            rows_copy(px_rows + py_rows + 8 * gy + 4 * gx, 8 // parts, (step_to[gx], step_to[gy], 0))
+            rows_copy(pair + 8 * gy + 4 * gx, 8 // parts, (step_to[gx], step_to[gy], 0))
     for gx in ways:
         rows_copy(px_rows // 2 * gx, px_rows // parts, (step_to[gx], 0, 0))
     for gy in (0, 1):
@@ -504,7 +520,7 @@
             lax.fori_loop(1, ndev, send, 0)
 
     pieces = mix_rows(reach_rows[...], here)
-    pieces = pieces[0 : 8 * deep] + pieces[8 * deep :]
+    pieces = doubled(pieces, 8 * deep)
     blocks = [part.astype(jnp.float32) for part in three(pieces)]
 
     def stack(first, last):
@@ -523,22 +539,37 @@
     spread(msg, gath.at[slot], g_send, g_recv)
     gath[slot] = msg[...]
     sums = finish()
+    quarter = own // 4
+
+    def level_rows(v, columns):
+        return (
+            mix_rows(rows1[:, columns], v[:, 0:LANES]),
+            doubled(mix_rows(rows2[:, columns], v[:, LANES:]), quarter),
+        )
+
+    o1s[...], early = level_rows(mix_lanes(here, lanes12[...]), pl.ds(0, own))
+    o2s[...] = early.reshape(o2s.shape)
     settle(grown.at[pl.ds(0, sent_rows)], m_send, m_recv)
 
     for g in (0, 1):
-        v = jnp.where(lane2 < px_rows // 2, t2r[g, 0], t2r[g, 0 if alone else 1])
-        v = jnp.where(lane2 < px_rows, v, jnp.where(lane2 < px_rows + py_rows // 2, t2r[g, 2], t2r[g, 3]))
+        place_in = lane2 % pair
+        v = jnp.where(place_in < ay, t2r[g, 0], t2r[g, 0 if alone else 1])
+        v = jnp.where(place_in < px_rows, v, jnp.where(place_in < px_rows + ax, t2r[g, 2], t2r[g, 3]))
         hz[g, :, pl.ds(own, LANES)] = v
         u = []
         for gy in (0, 1):
             u.append(jnp.where(lane2 % 8 < 4, t3r[g, gy, 0], t3r[g, gy, 0 if alone else 1]))
         v = jnp.where(lane2 < 8, u[0], u[1])
         hz[g, :, pl.ds(own + LANES, LANES)] = jnp.where(lane2 < 16, v, 0.0)
-    rim_rows = columns(jnp.concatenate((hz[0], hz[1]), axis=0), rim1[...])
-    wide = mix_lanes(grown[...], lanes1[...]) + rim_rows[0 : own + extra]
-    first = mix_rows(rows1[...], wide)
-    second = mix_lanes(mix_rows(rows2[...], first), lanes2[...])
-    o1s[...] = first[0:own]
+    rim_rows = columns(jnp.concatenate((hz[0], hz[1]), axis=0), rim12[...])
+    got = grown[pl.ds(own, pair + 16), :]
+    outer = mix_lanes(got, lanes12[...])
+    outer = (outer[0:pair], mix_lanes(got[0:pair], odd_lanes12[...]), outer[pair:])
+    outer = jnp.concatenate(outer, axis=0) + rim_rows[own : own + extra]
+    late = level_rows(jnp.concatenate((rim_rows[0:own], outer), axis=0), pl.ds(0, own + extra))
+    first = o1s[...] + late[0]
+    second = o2s[...].reshape(quarter, LANES) + late[1]
+    o1s[...] = first
     o2s[...] = second.reshape(o2s.shape)
 
     def tally(v, level, ny):
@@ -549,7 +580,7 @@
         small = shrink(v, thresh(level))
         return [total(jnp.where(use, v * v, 0.0)), total(jnp.where(use, jnp.abs(small), 0.0))]
 
-    sums += tally(first[0:own], 1, ay) + tally(second, 2, ay // 2)
+    sums += tally(first, 1, ay) + tally(second, 2, ay // 2)
 
     def place(source, level):
         s = 2**level
@@ -666,7 +697,7 @@
         pltpu.SemaphoreType.DMA,
         pltpu.SemaphoreType.DMA,
         *(pltpu.VMEM(shape, jnp.float32) for shape in (
-            (own + extra, LANES), (extra, LANES), (2, 2, own + 2 * LANES), (2, 2, own + 2 * LANES),
+            (own + lx + ly + 16, LANES), (lx + ly + 16, LANES), (2, 2, own + 2 * LANES), (2, 2, own + 2 * LANES),
             (2, 4, 2, LANES), (2, 2, 2, 2, LANES), (own, LANES), (lx // 4, ly // 4, LANES),
         )),
         pltpu.SemaphoreType.DMA,

time: 22.5 us -> 22.4 us (level)
  no operation moved by 1% of the time
where the time goes in v6:
time: 22.4 us; the launch traced here: 22.2 us
  Pallas kernels  21.6 us (96%)
  between operations  0.64 us (3%)
    pallas_call x1, Pallas kernels, shards(): pl.pallas_call(functools.partial(kernel, sizes, cells), out_shape=(pltpu....  20.7 us
    pallas_call x1, Pallas kernels, shards(): pl.pallas_call(deliver, out_shape=(jax.ShapeDtypeStruct(fields.shape, jnp...  0.83 us

profile of v6, /device:TPU:0, one launch (start us, length us, event | category | flops | bytes accessed | tf_op | source)
XLA Modules:
  0.0 22.2 jit_solution(1643421524216162797)
XLA Ops:
  0.6 20.7 %shard_map.167 = (f32[1,32,32,128]{3,2,1,0:T(8,128)S(1)}, f32[2,1,5]{2,1,0:T(1,128)S(1)}) custom-call(s32[5]{0:T(128)} %exps_in.1, f32[1,32,32,128]{3,2,1,0:T(8,128)} %field_in.1, f32[2,128,392]{2,1,0:T(8,128)} %constant.28.clone.rows_in, f32[2,128,128]{2,1,0:T(8,128)} %constant.29.clone.lanes_in, bf16[128,128]{1,0:T(8,128)(2,1)} %constant.30.clone.rest_0_, ...), custom_call_target="tpu_custom_call" | custom-call | tf_op jit(solution)/shard_map/pallas_call | solution.py:722
  21.4 0.8 %shard_map.168 = (f32[1,32,32,128]{3,2,1,0:T(8,128)}, f32[2,1,5]{2,1,0:T(1,128)}) custom-call(f32[1,32,32,128]{3,2,1,0:T(8,128)S(1)} %get-tuple-element.4.held, f32[2,1,5]{2,1,0:T(1,128)S(1)} %get-tuple-element.5.held_stats), custom_call_target="tpu_custom_call" | custom-call | tf_op jit(solution)/shard_map/pallas_call | solution.py:736

commit v7 on v6

--- a/solution.py
+++ b/solution.py
@@ -14,7 +14,7 @@
 LANES = 128
 CHUNKS = 4
 BUFFERS = 18
-TABLES = 12
+TABLES = 14
 BATCH = 8
 ROUNDS = 2
 VMEM_LIMIT = 58_720_256
@@ -124,9 +124,9 @@
     place = np.zeros((16, LANES))
     for z in range(2):
         for x in range(2):
-            edges[2 * z + x, 1 + z :: q] = ends[x]
-            for part in range(3):
-                place[4 * part + 2 * z + x, (LANES - q) * x + 1 + z] = 1.0
+            edges[2 * z + x, 2 - 2 * z :: q] = ends[x]
+            for lane in ((2,), (0, 1))[z]:
+                place[2 * z + x : 12 : 4, (LANES - q) * x + lane] = 1.0
     result = (lift_line(LANES)[:, :LANES].T, edges, place)
     return tuple(table.astype(jnp.bfloat16) for table in result)
 
@@ -136,6 +136,11 @@
     sent_x, first_x, second_x = line_tables(ax)
     sent_y, first_y, second_y = line_tables(ay)
     sent_z, first_z, second_z = line_tables(az)
+    finer = lift_line(2 * ay)
+    low, high = finer[0, 2 * ay], finer[2 * ay - 2, 2 * ay + 1]
+    after = sent_y[2, 0] * first_y[:, ay + 2] + sent_y[3, 0] * first_y[:, ay + 3]
+    before = sent_y[0, ay - 1] * first_y[:, ay] + sent_y[1, ay - 1] * first_y[:, ay + 1]
+    first_y = np.concatenate((first_y, np.stack((low * after, high * before), axis=1)), axis=1)
     own = [(x, y) for x in range(ax) for y in range(ay)]
     corners = [(x, 2 * g + y) for g in range(2) for x in range(4) for y in range(2)]
     extra = []
@@ -143,6 +148,11 @@
         extra += [(ax + k, y) for k in (start, start + 2) for y in range(ay)]
         extra += [(x, ay + k) for k in (start, start + 2) for x in range(ax)]
     extra += [(ax + x, ay + y) for x, y in corners]
+    pair = 2 * ax + 2 * ay
+    by_x = extra[: 2 * ay] + extra[pair : pair + 2 * ay]
+    by_y = extra[2 * ay : pair] + extra[pair + 2 * ay :]
+    extra += [(x, ay + 4 + k) for k in range(2) for x in range(ax)]
+    extra += [(ax + x, ay + 4 + k) for x in range(4) for k in range(2)]
     taken = np.array(own + extra)
     given = own + [(ax + k, y) for k in range(2) for y in range(0, ay, 2)]
     given += [(x, ay + k) for k in range(2) for x in range(0, ax, 2)]
@@ -150,13 +160,17 @@
     height = -(-len(given) // 16) * 16
 
     whole_x, whole_y = np.concatenate((np.eye(ax), sent_x)), np.concatenate((np.eye(ay), sent_y))
-    ex, ey = np.array(extra).T
     ox, oy = np.array(own).T
-    send_rows = whole_x[np.ix_(ex, ox)] * whole_y[np.ix_(ey, oy)]
+    sends = []
+    for kinds in (by_y, by_x):
+        ex, ey = np.array(kinds).T
+        sends.append(whole_x[np.ix_(ex, ox)] * whole_y[np.ix_(ey, oy)])
+    sends.append(np.zeros((16, 2 * ax)))
+    sends[2][:8] = np.kron(sent_x, np.eye(2)).reshape(8, ax, 2).transpose(0, 2, 1).reshape(8, -1)
     gx, gy = np.array(given).T
     tx, ty = taken.T
-    rows = np.zeros((height, len(taken)))
-    rows[: len(given)] = first_x[np.ix_(gx, tx)] * first_y[np.ix_(gy, ty)]
+    rows = np.zeros((height, len(taken) + 8))
+    rows[: len(given), : len(taken)] = first_x[np.ix_(gx, tx)] * first_y[np.ix_(gy, ty)]
 
     def spot(at, n):
         return np.where(at >= n, n // 2 + at - n, at // 2)
@@ -183,7 +197,7 @@
     last = np.concatenate(cut_table(last @ rows))
     along = np.concatenate((along, along @ along_last), axis=1)
     rim = np.concatenate((rim, rim @ along_last), axis=1)
-    result = (send_rows, rows[: len(own)], last, send_lanes, along, np.roll(along, 1, 0), rim)
+    result = (*sends, rows[: len(own)], last, send_lanes, along, np.roll(along, 1, 0), rim)
     return tuple(table.astype(jnp.bfloat16) for table in result)
 
 
@@ -310,7 +324,8 @@
     alone = nx == 2
     ways = (0,) if alone else (0, 1)
     (xs, xr, ys, yr, es, er, yl, zs, zr, ds, dr, ts, txr, tcr, rim, work, send_sem, recv_sem) = scratch[:BUFFERS]
-    grown, sent, side, hz, t2r, t3r, o1s, o2s, m_send, m_recv = scratch[BUFFERS : BUFFERS + 10]
+    middle = scratch[BUFFERS : BUFFERS + 15]
+    grown, ghost, sent, edge1, side, hz, xzr, t2r, t3r, o1s, o2s, m_send, m_recv, y_send, y_recv = middle
     fine_lanes, fine_edges, fine_place, reach_rows, reach_lanes, *tables = tables
     src = field.at[0]
     px, n = src.shape[0], src.shape[1]
@@ -333,7 +348,9 @@
     packed = jnp.zeros((n, LANES), jnp.float32)
     for x in range(px):
         packed = jnp.where(lane // q == x, roll(src[x], q * x + 2, 1), packed)
-    packed = jnp.where(lane % q == 1, packed - 0.5 * roll(packed, 1, 1), packed)
+    odd_end = roll(packed - 0.5 * roll(packed, 1, 1), 1, 1)
+    even_end = jnp.where(lane % q == 1, roll(packed, -1, 1), roll(packed, -2, 1))
+    packed = jnp.where(lane % q == 2, odd_end, even_end)
     zs[...] = packed
     ds[0], ds[1] = ends(packed)
     for load in loads[2:5]:
@@ -347,30 +364,29 @@
         ts[g, :, pl.ds(0, n + 8)] = edges[2 * g : 2 * g + 2]
 
     pl.semaphore_wait(barrier, len(greeted))
-    copies = []
+    along_y, others = [], []
     for g in (0, 1):
         dz = step_to[g]
         for gx in ways:
             for gy in (0, 1):
-                copies.append((ts.at[g], tcr.at[g, gy, gx], (step_to[gx], step_to[gy], dz)))
-            copies.append((ts.at[g], txr.at[g, gx], (step_to[gx], 0, dz)))
+                along_y.append((ts.at[g], tcr.at[g, gy, gx], (step_to[gx], step_to[gy], dz)))
+            others.append((ts.at[g], txr.at[g, gx], (step_to[gx], 0, dz)))
         for gy in (0, 1):
-            copies.append((ds.at[gy], dr.at[2 * g + gy], (0, step_to[gy], dz)))
+            along_y.append((ds.at[gy], dr.at[2 * g + gy], (0, step_to[gy], dz)))
     for gx in (0, 1):
         for gy in (0, 1):
-            copies.append((es.at[2 * gx + gy], er.at[2 * gx + gy], (step_to[gx], step_to[gy], 0)))
-    for g in (0, 1):
-        copies.append((xs.at[g], xr.at[g], (step_to[g], 0, 0)))
-    for g in (0, 1):
-        copies.append((ys.at[g], yr.at[g], (0, step_to[g], 0)))
-    for g in (0, 1):
-        copies.append((zs, zr.at[g], (0, 0, step_to[g])))
-    sent_rows = launch(copies, send_sem, recv_sem)
+            along_y.append((es.at[2 * gx + gy], er.at[2 * gx + gy], (step_to[gx], step_to[gy], 0)))
+    for g in (0, 1):
+        along_y.append((ys.at[g], yr.at[g], (0, step_to[g], 0)))
+    for g in (0, 1):
+        others.append((xs.at[g], xr.at[g], (step_to[g], 0, 0)))
+    for g in (0, 1):
+        others.append((zs, zr.at[g], (0, 0, step_to[g])))
+    y_rows = launch(along_y, y_send, y_recv)
+    sent_rows = launch(others, send_sem, recv_sem)
     settle(grown.at[pl.ds(0, sent_rows)], send_sem, recv_sem)
 
     lane2, row2 = iota((2, LANES), 1), iota((2, LANES), 0)
-    for g in (0, 1):
-        yl[g] = lift_rows(yr[g], er[g], er[2 + g])
 
     def both(ref):
         return ref[0] if alone else jnp.where(row2 == 0, ref[0], ref[1])
@@ -380,37 +396,56 @@
         pieces.append(jnp.zeros_like(top))
         return mix(jnp.concatenate(pieces, axis=0).astype(jnp.bfloat16), table, ((0,), (0,)))
 
-    tops = []
-    for g in (0, 1):
-        v = jnp.where(lane2 == n, both(tcr.at[g, 0]), both(tcr.at[g, 1]))
-        v = jnp.where(lane2 < n, both(txr.at[g]), v)
-        tops.append(jnp.where(lane2 < n + 2, v, 0.0))
-    beside = columns(jnp.concatenate(tops, axis=0), fine_place[...])[0 : n + 8]
-
     def kinds(a, b):
-        return jnp.where(iota(a.shape, 1) % q == 1, a, b)
-
-    lower = under((kinds(dr[0], dr[2]), kinds(dr[1], dr[3])))
-    v = lift_groups(jnp.concatenate((kinds(zr[0], zr[1]), lower), axis=0), beside, q)
-    v = lift_rows(v[0:n], v[n : n + 1], v[n + 1 : n + 2])
-    v = jnp.where(lane % q == 2, roll(v, 1, 1), jnp.where(lane % q == 1, roll(v, -1, 1), roll(v, -2, 1)))
-    rim[...] = v
-    border = jnp.concatenate((rim[pl.ds(0, half, stride=2), :], rim[pl.ds(1, half, stride=2), :]), axis=0)
-    share = jnp.where(lane == LANES - 1, -0.5, jnp.where(lane == LANES - 2, -0.125, jnp.where(lane == 0, 0.25, 0.0)))
+        return jnp.where(iota(a.shape, 1) % q == 2, a, b)
+
+    lane_half = iota((half, LANES), 1)
+    share = jnp.where(lane_half == LANES - 2, -0.125, jnp.where(lane_half == 0, 0.25, 0.0))
+    share = jnp.where(lane_half == LANES - 1, -0.5, share)
     level_thresh = thresh(0)
-    inner = (iota((n, LANES), 0) < half) & (lane % 2 == 0)
     row = iota((half, LANES), 0)
+    ax, ay = px // 2, half
+    own = ax * ay
+    px_rows, py_rows = 2 * ay, 2 * ax
+    pair = px_rows + py_rows
+    send_y, send_x, send_q, rows1, rows2, send_lanes, lanes12, odd_lanes12, rim12 = tables
+    none = jnp.zeros((1, LANES), jnp.float32)
 
     def halves(ref, x):
         return [ref[x, pl.ds(start, half, stride=2), :] for start in (0, 1)]
 
-    def lift_halves(v, x):
+    def stored(x):
+        return [work[x, 0:half], work[x, half:]]
+
+    def lift_halves(v, below, above):
         even, odd = v
-        after = jnp.where(row == half - 1, yl[1, x : x + 1, :], roll(even, -1, 0))
+        after = jnp.where(row == half - 1, above, roll(even, -1, 0))
         detail = odd - 0.5 * (even + after)
-        before = jnp.where(row == 0, yl[0, x : x + 1, :] - 0.5 * even, roll(detail, 1, 0))
+        before = jnp.where(row == 0, below - 0.5 * even, roll(detail, 1, 0))
         return [even + 0.25 * (before + detail), detail]
 
+    def lift_last(stack, border):
+        whole = mix_lanes(jnp.concatenate([v for v, _, _ in stack], axis=0), fine_lanes[...])
+        for i, (_, x, kind) in enumerate(stack):
+            yield x, kind, whole[half * i : half * i + half] + roll(border[kind], LANES - 2 - q * x, 1) * share
+
+    def sideways(parts, target):
+        edges = sum(mix(send_lanes[...], part, ((1,), (1,))) for part in three(jnp.concatenate(parts, axis=0)))
+        for g in (0, 1):
+            target[g, :, pl.ds(target.shape[2] - LANES, LANES)] = jnp.zeros((2, LANES), jnp.float32)
+            target[g, :, pl.ds(0, edges.shape[1])] = edges[2 * g : 2 * g + 2]
+
+    def both_kinds(a, b):
+        return jnp.where(iota(a.shape, 1) % 2 == 0, a, roll(b, 1, 1))
+
+    for load in loads[5 : 2 + TABLES]:
+        load.wait()
+    tops = [jnp.where(lane2 < n, both(txr.at[g]), 0.0) for g in (0, 1)]
+    beside = columns(jnp.concatenate(tops, axis=0), fine_place[...])[0:n]
+    v = lift_groups(kinds(zr[0], zr[1]), beside, q)
+    outer_rims = ends(v)
+    rim[...] = lift_rows(v, none, none)
+    border = [rim[pl.ds(0, half, stride=2), :]]
     even = halves(src, 0)
     before = [p - 0.5 * e for p, e in zip(halves(xr, 0), even)]
     stack = []
@@ -418,80 +453,119 @@
         after = halves(src, 2 * k + 2) if 2 * k + 2 < px else halves(xr, 1)
         detail = [o - 0.5 * (e + a) for o, e, a in zip(halves(src, 2 * k + 1), even, after)]
         smooth = [e + 0.25 * (b + d) for e, b, d in zip(even, before, detail)]
-        stack += lift_halves(smooth, 2 * k) + lift_halves(detail, 2 * k + 1)
+        work[2 * k, 0:half], work[2 * k, half:] = smooth
+        work[2 * k + 1, 0:half], work[2 * k + 1, half:] = detail
+        stack.append((lift_halves(smooth, none, none)[0], 2 * k, 0))
         even, before = after, detail
-        if len(stack) == 2 * BATCH:
-            wide = mix_lanes(jnp.concatenate(stack, axis=0), fine_lanes[...])
-            for i in range(BATCH):
-                x = 2 * k + 2 - BATCH + i
-                v = wide[n * i : n * i + n] + roll(border, LANES - 2 - q * x, 1) * share
-                work[x] = v
-                if x % 2 == 0:
-                    grown[pl.ds(x // 2 * half, half), :] = v[0:half]
+        if len(stack) == BATCH:
+            for x, _, v in lift_last(stack, border):
+                ghost[pl.ds(x // 2 * half, half), :] = v
             stack = []
-
-    def finish():
-        energy = kept = jnp.zeros((n, LANES), jnp.float32)
-        for x in range(px):
-            v = work[x]
-            small = shrink(v, level_thresh)
-            if x % 2 == 0:
-                energy += jnp.where(inner, 0.0, v * v)
-                kept += jnp.where(inner, 0.0, jnp.abs(small))
-            else:
-                energy += v * v
-                kept += jnp.abs(small)
-            for start in (0, 1):
-                out[0, x, pl.ds(start, half, stride=2), :] = small[half * start : half * start + half]
-        return [total(energy), total(kept)]
-
-    ax, ay = px // 2, n // 2
-    own = ax * ay
-    send_rows, rows1, rows2, send_lanes, lanes12, odd_lanes12, rim12 = tables
-    for load in loads[5 : 2 + TABLES]:
-        load.wait()
-    here = grown[0:own]
-    halo = mix_rows(send_rows[...], here)
-    px_rows, py_rows = 2 * ay, 2 * ax
-    pair = px_rows + py_rows
-    second_kind = roll(halo[pair : 2 * pair], 1, 1)
-    sent[0:pair] = jnp.where(iota(second_kind.shape, 1) % 2 == 0, halo[0:pair], second_kind)
-    sent[pair:] = halo[2 * pair :]
-    edges = sum(
-        mix(send_lanes[...], part, ((1,), (1,)))
-        for part in three(jnp.concatenate((here, halo), axis=0))
-    )
-    extra = halo.shape[0]
-    for g in (0, 1):
-        side[g, :, pl.ds(own, 2 * LANES)] = jnp.zeros((2, 2 * LANES), jnp.float32)
-        side[g, :, pl.ds(0, own + extra)] = edges[2 * g : 2 * g + 2]
-
+    beyond = [ends(xr[g]) for g in (0, 1)]
+    raw = []
+    for g in (0, 1):
+        yl[g] = lift_rows(ys[g], beyond[0][g], beyond[1][g])
+        raw.append(yl[g, pl.ds(0, ax, stride=2), :])
+    raw = mix_lanes(jnp.concatenate(raw, axis=0), fine_lanes[...])
+    turned = []
+    for v in outer_rims:
+        v = jnp.broadcast_to(v, (8, LANES))
+        for start in range(0, ax, 8):
+            tile = jnp.zeros((8, LANES), jnp.float32)
+            for i in range(8):
+                tile = jnp.where(row8 == i, roll(v, LANES - 2 - 2 * q * (start + i), 1), tile)
+            turned.append(tile)
+    raw = raw + jnp.concatenate(turned, axis=0) * share[0:1]
+    grown[pl.ds(own + pair + 16, py_rows), :] = raw
+    grown[pl.ds(own + pair + 24 + py_rows, 8), :] = jnp.zeros((8, LANES), jnp.float32)
+
+    halo = mix_rows(send_y[...], ghost[...])
+    halo = (halo[0:py_rows], halo[py_rows : 2 * py_rows], halo[2 * py_rows :])
+    sent[px_rows:pair] = both_kinds(halo[0], halo[1])
+    sent[pair : pair + 16] = halo[2]
+    blank = jnp.zeros((px_rows, LANES), jnp.float32)
+    sideways((blank, halo[0], blank, halo[1], halo[2]), edge1)
     copies = []
-    for g in (0, 1):
-        dz = step_to[g]
-        tail = pl.ds(own + LANES, LANES)
+
+    def rows_copy(start, size, to):
+        copies.append((sent.at[pl.ds(start, size)], grown.at[pl.ds(own + start, size)], to))
+
+    parts = len(ways)
+    for g in (0, 1):
         for gy in (0, 1):
             for gx in ways:
-                copies.append((side.at[g, :, tail], t3r.at[g, gy, gx], (step_to[gx], step_to[gy], dz)))
-        middle = pl.ds(own, LANES)
-        for gx in ways:
-            copies.append((side.at[g, :, middle], t2r.at[g, gx], (step_to[gx], 0, dz)))
-        for gy in (0, 1):
-            copies.append((side.at[g, :, middle], t2r.at[g, 2 + gy], (0, step_to[gy], dz)))
-        copies.append((side.at[g, :, pl.ds(0, own)], hz.at[g, :, pl.ds(0, own)], (0, 0, dz)))
-
-    def rows_copy(start, size, to):
-        copies.append((sent.at[pl.ds(start, size)], grown.at[pl.ds(own + start, size)], to))
-
-    parts = len(ways)
+                copies.append((edge1.at[g, :, pl.ds(LANES, LANES)], t3r.at[g, gy, gx], (step_to[gx], step_to[gy], step_to[g])))
+            copies.append((edge1.at[g, :, pl.ds(0, LANES)], t2r.at[g, gy], (0, step_to[gy], step_to[g])))
     for gy in (0, 1):
         for gx in ways:
             rows_copy(pair + 8 * gy + 4 * gx, 8 // parts, (step_to[gx], step_to[gy], 0))
+    for gy in (0, 1):
+        rows_copy(px_rows + ax * gy, ax, (0, step_to[gy], 0))
+    sent_rows = launch(copies, m_send, m_recv)
+    settle(grown.at[pl.ds(0, y_rows)], y_send, y_recv)
+
+    tops = []
+    for g in (0, 1):
+        yl[g] = lift_rows(yr[g], er[g], er[2 + g])
+        v = jnp.where(lane2 == n, both(tcr.at[g, 0]), both(tcr.at[g, 1]))
+        v = jnp.where(lane2 < n, both(txr.at[g]), v)
+        tops.append(jnp.where(lane2 < n + 2, v, 0.0))
+    beside = columns(jnp.concatenate(tops, axis=0), fine_place[...])[0 : n + 8]
+    lower = under((kinds(dr[0], dr[2]), kinds(dr[1], dr[3])))
+    v = lift_groups(jnp.concatenate((kinds(zr[0], zr[1]), lower), axis=0), beside, q)
+    v = lift_rows(v[0:n], v[n : n + 1], v[n + 1 : n + 2])
+    rim[...] = v
+    border = [rim[pl.ds(start, half, stride=2), :] for start in (0, 1)]
+    stack = []
+    for x in range(0, px, 2):
+        smooth = lift_halves(stored(x), yl[0, x : x + 1, :], yl[1, x : x + 1, :])
+        work[x, half:] = smooth[1]
+        stack.append((smooth[0], x, 0))
+        if len(stack) == BATCH:
+            for at, _, v in lift_last(stack, border):
+                work[at, 0:half] = v
+                grown[pl.ds(at // 2 * half, half), :] = v
+            stack = []
+
+    def finish():
+        energy = kept = jnp.zeros((half, LANES), jnp.float32)
+        for start in range(0, px, 4):
+            stack, ready = [], []
+            for x in range(start, start + 4, 2):
+                ready.append((x, 0, work[x, 0:half]))
+                stack.append((work[x, half:], x, 1))
+                lifted = lift_halves(stored(x + 1), yl[0, x + 1 : x + 2, :], yl[1, x + 1 : x + 2, :])
+                stack += [(lifted[0], x + 1, 0), (lifted[1], x + 1, 1)]
+            for x, kind, v in (*ready, *lift_last(stack, border)):
+                small = shrink(v, level_thresh)
+                out[0, x, pl.ds(kind, half, stride=2), :] = small
+                square, size = v * v, jnp.abs(small)
+                if x % 2 == 0 and kind == 0:
+                    square, size = (jnp.where(lane_half % 2 == 0, 0.0, u) for u in (square, size))
+                energy += square
+                kept += size
+        return [total(energy), total(kept)]
+
+    here = grown[0:own]
+    halo = mix_rows(send_x[...], here)
+    corner = mix_rows(send_q[...], raw)[0:8]
+    sent[0:px_rows] = both_kinds(halo[0:px_rows], halo[px_rows:])
+    sent[pair + 16 :] = corner
+    blank = jnp.zeros((py_rows, LANES), jnp.float32)
+    filled = jnp.zeros((16, LANES), jnp.float32)
+    sideways((here, halo[0:px_rows], blank, halo[px_rows:], blank, filled, raw, corner, filled[0:8]), side)
+    copies = []
+    for g in (0, 1):
+        for gx in ways:
+            copies.append((side.at[g, :, pl.ds(own, 2 * LANES)], xzr.at[g, gx], (step_to[gx], 0, step_to[g])))
+        copies.append((side.at[g], hz.at[g], (0, 0, step_to[g])))
     for gx in ways:
-        rows_copy(px_rows // 2 * gx, px_rows // parts, (step_to[gx], 0, 0))
-    for gy in (0, 1):
-        rows_copy(px_rows + py_rows // 2 * gy, py_rows // 2, (0, step_to[gy], 0))
-    sent_rows = launch(copies, m_send, m_recv)
+        size = 8 // parts
+        at = own + pair + 16 + py_rows + size * gx
+        copies.append((sent.at[pl.ds(pair + 16 + size * gx, size)], grown.at[pl.ds(at, size)], (step_to[gx], 0, 0)))
+        rows_copy(ay * gx, px_rows // parts, (step_to[gx], 0, 0))
+    sent_rows += launch(copies, m_send, m_recv)
+    extra = 2 * pair + 16 + py_rows + 16
 
     spots = nx * ny
     slot = (me[2] * nx + me[0]) * ny + me[1]
@@ -552,17 +626,21 @@
     settle(grown.at[pl.ds(0, sent_rows)], m_send, m_recv)
 
     for g in (0, 1):
+        across = (xzr.at[g, 0], xzr.at[g, 0 if alone else 1])
         place_in = lane2 % pair
-        v = jnp.where(place_in < ay, t2r[g, 0], t2r[g, 0 if alone else 1])
-        v = jnp.where(place_in < px_rows, v, jnp.where(place_in < px_rows + ax, t2r[g, 2], t2r[g, 3]))
+        v = jnp.where(place_in < ay, across[0][:, 0:LANES], across[1][:, 0:LANES])
+        v = jnp.where(place_in < px_rows, v, jnp.where(place_in < px_rows + ax, t2r[g, 0], t2r[g, 1]))
         hz[g, :, pl.ds(own, LANES)] = v
         u = []
         for gy in (0, 1):
             u.append(jnp.where(lane2 % 8 < 4, t3r[g, gy, 0], t3r[g, gy, 0 if alone else 1]))
         v = jnp.where(lane2 < 8, u[0], u[1])
-        hz[g, :, pl.ds(own + LANES, LANES)] = jnp.where(lane2 < 16, v, 0.0)
+        w = jnp.where(lane2 < 20 + py_rows, across[0][:, LANES:], across[1][:, LANES:])
+        w = jnp.where(lane2 < 16 + py_rows, hz[g, :, pl.ds(own + LANES, LANES)], w)
+        v = jnp.where(lane2 < 16, v, jnp.where(lane2 < 24 + py_rows, w, 0.0))
+        hz[g, :, pl.ds(own + LANES, LANES)] = v
     rim_rows = columns(jnp.concatenate((hz[0], hz[1]), axis=0), rim12[...])
-    got = grown[pl.ds(own, pair + 16), :]
+    got = grown[pl.ds(own, extra - pair), :]
     outer = mix_lanes(got, lanes12[...])
     outer = (outer[0:pair], mix_lanes(got[0:pair], odd_lanes12[...]), outer[pair:])
     outer = jnp.concatenate(outer, axis=0) + rim_rows[own : own + extra]
@@ -697,9 +775,12 @@
         pltpu.SemaphoreType.DMA,
         pltpu.SemaphoreType.DMA,
         *(pltpu.VMEM(shape, jnp.float32) for shape in (
-            (own + lx + ly + 16, LANES), (lx + ly + 16, LANES), (2, 2, own + 2 * LANES), (2, 2, own + 2 * LANES),
-            (2, 4, 2, LANES), (2, 2, 2, 2, LANES), (own, LANES), (lx // 4, ly // 4, LANES),
+            (own + 2 * lx + ly + 32, LANES), (own, LANES), (lx + ly + 24, LANES), (2, 2, 2 * LANES),
+            (2, 2, own + 2 * LANES), (2, 2, own + 2 * LANES), (2, 2, 2, 2 * LANES), (2, 2, 2, LANES),
+            (2, 2, 2, 2, LANES), (own, LANES), (lx // 4, ly // 4, LANES),
         )),
+        pltpu.SemaphoreType.DMA,
+        pltpu.SemaphoreType.DMA,
         pltpu.SemaphoreType.DMA,
         pltpu.SemaphoreType.DMA,
     ]

time: 22.4 us -> 21.8 us (0.973)
  Pallas kernels: 21.6 us -> 21 us
    pallas_call x1, Pallas kernels: 20.7 us -> 20.2 us  [shards(): pl.pallas_call(functools.partial(kernel, sizes, cells), out_shape=(pltpu....]
where the time goes in v7:
time: 21.8 us; the launch traced here: 21.6 us
  Pallas kernels  21 us (96%)
  between operations  0.64 us (3%)
    pallas_call x1, Pallas kernels, shards(): pl.pallas_call(functools.partial(kernel, sizes, cells), out_shape=(pltpu....  20.2 us
    pallas_call x1, Pallas kernels, shards(): pl.pallas_call(deliver, out_shape=(jax.ShapeDtypeStruct(fields.shape, jnp...  0.83 us

profile of v7, /device:TPU:0, one launch (start us, length us, event | category | flops | bytes accessed | tf_op | source)
XLA Modules:
  0.0 21.6 jit_solution(4361461166969196271)
XLA Ops:
  0.6 20.2 %shard_map.185 = (f32[1,32,32,128]{3,2,1,0:T(8,128)S(1)}, f32[2,1,5]{2,1,0:T(1,128)S(1)}) custom-call(s32[5]{0:T(128)} %exps_in.1, f32[1,32,32,128]{3,2,1,0:T(8,128)} %field_in.1, f32[2,128,392]{2,1,0:T(8,128)} %constant.32.clone.rows_in, f32[2,128,128]{2,1,0:T(8,128)} %constant.33.clone.lanes_in, bf16[128,128]{1,0:T(8,128)(2,1)} %constant.34.clone.rest_0_, ...), custom_call_target="tpu_custom_call" | custom-call | tf_op jit(solution)/shard_map/pallas_call | solution.py:803
  20.8 0.8 %shard_map.186 = (f32[1,32,32,128]{3,2,1,0:T(8,128)}, f32[2,1,5]{2,1,0:T(1,128)}) custom-call(f32[1,32,32,128]{3,2,1,0:T(8,128)S(1)} %get-tuple-element.4.held, f32[2,1,5]{2,1,0:T(1,128)S(1)} %get-tuple-element.5.held_stats), custom_call_target="tpu_custom_call" | custom-call | tf_op jit(solution)/shard_map/pallas_call | solution.py:817

commit v8 on v7

--- a/solution.py
+++ b/solution.py
@@ -13,7 +13,7 @@
 LEVELS = 5
 LANES = 128
 CHUNKS = 4
-BUFFERS = 18
+BUFFERS = 20
 TABLES = 14
 BATCH = 8
 ROUNDS = 2
@@ -59,8 +59,10 @@
         both = mx[gx[:, None], from_x[None]] * my[gy[:, None], from_y[None]]
         along = np.zeros((LANES, LANES))
         along[np.ix_(np.arange(len(from_z)), lanes)] = mz[:, from_z].T
-        result.append((both.astype(np.float32), along.astype(np.float32)))
-    return [np.stack(pair) for pair in zip(*result)]
+        result.append((np.pad(both, ((0, 0), (0, -both.shape[1] % 16))), along.astype(jnp.bfloat16)))
+    (one, along_one), (two, along_two) = result
+    rows = np.concatenate((one.astype(jnp.bfloat16), *cut_table(two)))
+    return rows, np.stack((along_one, along_two))
 
 
 def cut_table(table):
@@ -323,9 +325,9 @@
     step_to = (1, -1)
     alone = nx == 2
     ways = (0,) if alone else (0, 1)
-    (xs, xr, ys, yr, es, er, yl, zs, zr, ds, dr, ts, txr, tcr, rim, work, send_sem, recv_sem) = scratch[:BUFFERS]
+    (xs, xh, xe, xr, ys, yr, es, er, yl, zs, zr, ds, dr, ts, txr, tcr, rim, work, send_sem, recv_sem) = scratch[:BUFFERS]
     middle = scratch[BUFFERS : BUFFERS + 15]
-    grown, ghost, sent, edge1, side, hz, xzr, t2r, t3r, o1s, o2s, m_send, m_recv, y_send, y_recv = middle
+    grown, lifted, sent, edge1, side, hz, xzr, t2r, t3r, o1s, o2s, m_send, m_recv, y_send, y_recv = middle
     fine_lanes, fine_edges, fine_place, reach_rows, reach_lanes, *tables = tables
     src = field.at[0]
     px, n = src.shape[0], src.shape[1]
@@ -339,11 +341,51 @@
     def under(pair):
         return jnp.where(row8 == 0, pair[0], jnp.where(row8 == 1, pair[1], 0.0))
 
+    lane_half = iota((half, LANES), 1)
+    share = jnp.where(lane_half == LANES - 2, -0.125, jnp.where(lane_half == 0, 0.25, 0.0))
+    share = jnp.where(lane_half == LANES - 1, -0.5, share)
+    level_thresh = thresh(0)
+    row = iota((half, LANES), 0)
+    ax, ay = px // 2, half
+    own = ax * ay
+    px_rows, py_rows = 2 * ay, 2 * ax
+    pair = px_rows + py_rows
+    send_y, send_x, send_q, rows1, rows2, send_lanes, lanes12, odd_lanes12, rim12 = tables
+    none = jnp.zeros((1, LANES), jnp.float32)
+
+    def halves(ref, x):
+        return [ref[x, pl.ds(start, half, stride=2), :] for start in (0, 1)]
+
+    def stored(x):
+        return [work[x, 0:half], work[x, half:]]
+
+    def lift_halves(v, below, above):
+        even, odd = v
+        after = jnp.where(row == half - 1, above, roll(even, -1, 0))
+        detail = odd - 0.5 * (even + after)
+        before = jnp.where(row == 0, below - 0.5 * even, roll(detail, 1, 0))
+        return [even + 0.25 * (before + detail), detail]
+
+    def lift_last(stack, border):
+        whole = mix_lanes(jnp.concatenate([v for v, _, _ in stack], axis=0), fine_lanes[...])
+        for i, (_, x, kind) in enumerate(stack):
+            yield x, kind, whole[half * i : half * i + half] + roll(border[kind], LANES - 2 - q * x, 1) * share
+
+    def sideways(parts, target):
+        edges = sum(mix(send_lanes[...], part, ((1,), (1,))) for part in three(jnp.concatenate(parts, axis=0)))
+        for g in (0, 1):
+            target[g, :, pl.ds(target.shape[2] - LANES, LANES)] = jnp.zeros((2, LANES), jnp.float32)
+            target[g, :, pl.ds(0, edges.shape[1])] = edges[2 * g : 2 * g + 2]
+
+    def both_kinds(a, b):
+        return jnp.where(iota(a.shape, 1) % 2 == 0, a, roll(b, 1, 1))
+
     planes = (src[px - 1] - 0.5 * src[px - 2], src[0])
     ys[0] = src[:, n - 1, :] - 0.5 * src[:, n - 2, :]
     ys[1] = src[:, 0, :]
     for gx in (0, 1):
         xs[gx] = planes[gx]
+        xh[gx, 0:half], xh[gx, half:] = lift_halves(halves(xs, gx), none, none)
         es[2 * gx], es[2 * gx + 1] = ends(planes[gx])
     packed = jnp.zeros((n, LANES), jnp.float32)
     for x in range(px):
@@ -379,11 +421,32 @@
     for g in (0, 1):
         along_y.append((ys.at[g], yr.at[g], (0, step_to[g], 0)))
     for g in (0, 1):
-        others.append((xs.at[g], xr.at[g], (step_to[g], 0, 0)))
+        ends_of = pl.ds(2 * g, 2)
+        others.append((es.at[ends_of], xe.at[ends_of], (step_to[g], 0, 0)))
+    for g in (0, 1):
+        others.append((xh.at[g, pl.ds(0, half)], xr.at[g, pl.ds(0, half)], (step_to[g], 0, 0)))
+        along_y.append((xh.at[g, pl.ds(half, half)], xr.at[g, pl.ds(half, half)], (step_to[g], 0, 0)))
     for g in (0, 1):
         others.append((zs, zr.at[g], (0, 0, step_to[g])))
-    y_rows = launch(along_y, y_send, y_recv)
+    y_rows = launch(along_y[:-2], y_send, y_recv)
     sent_rows = launch(others, send_sem, recv_sem)
+    y_rows += launch(along_y[-2:], y_send, y_recv)
+
+    for load in loads[5 : 2 + TABLES]:
+        load.wait()
+    even = halves(src, 0)
+    before = [-0.5 * e for e in even]
+    stack = []
+    for k in range(px // 2):
+        after = halves(src, 2 * k + 2) if 2 * k + 2 < px else [0.0, 0.0]
+        detail = [o - 0.5 * (e + a) for o, e, a in zip(halves(src, 2 * k + 1), even, after)]
+        smooth = [e + 0.25 * (b + d) for e, b, d in zip(even, before, detail)]
+        for x, v in ((2 * k, smooth), (2 * k + 1, detail)):
+            work[x, 0:half], work[x, half:] = lift_halves(v, none, none)
+        even, before = after, detail
+    for start in range(0, px, 2 * BATCH):
+        block = jnp.concatenate([work[x, 0:half] for x in range(start, start + 2 * BATCH, 2)], axis=0)
+        grown[pl.ds(start // 2 * half, BATCH * half), :] = mix_lanes(block, fine_lanes[...])
     settle(grown.at[pl.ds(0, sent_rows)], send_sem, recv_sem)
 
     lane2, row2 = iota((2, LANES), 1), iota((2, LANES), 0)
@@ -399,87 +462,20 @@
     def kinds(a, b):
         return jnp.where(iota(a.shape, 1) % q == 2, a, b)
 
-    lane_half = iota((half, LANES), 1)
-    share = jnp.where(lane_half == LANES - 2, -0.125, jnp.where(lane_half == 0, 0.25, 0.0))
-    share = jnp.where(lane_half == LANES - 1, -0.5, share)
-    level_thresh = thresh(0)
-    row = iota((half, LANES), 0)
-    ax, ay = px // 2, half
-    own = ax * ay
-    px_rows, py_rows = 2 * ay, 2 * ax
-    pair = px_rows + py_rows
-    send_y, send_x, send_q, rows1, rows2, send_lanes, lanes12, odd_lanes12, rim12 = tables
-    none = jnp.zeros((1, LANES), jnp.float32)
-
-    def halves(ref, x):
-        return [ref[x, pl.ds(start, half, stride=2), :] for start in (0, 1)]
-
-    def stored(x):
-        return [work[x, 0:half], work[x, half:]]
-
-    def lift_halves(v, below, above):
-        even, odd = v
-        after = jnp.where(row == half - 1, above, roll(even, -1, 0))
-        detail = odd - 0.5 * (even + after)
-        before = jnp.where(row == 0, below - 0.5 * even, roll(detail, 1, 0))
-        return [even + 0.25 * (before + detail), detail]
-
-    def lift_last(stack, border):
-        whole = mix_lanes(jnp.concatenate([v for v, _, _ in stack], axis=0), fine_lanes[...])
-        for i, (_, x, kind) in enumerate(stack):
-            yield x, kind, whole[half * i : half * i + half] + roll(border[kind], LANES - 2 - q * x, 1) * share
-
-    def sideways(parts, target):
-        edges = sum(mix(send_lanes[...], part, ((1,), (1,))) for part in three(jnp.concatenate(parts, axis=0)))
-        for g in (0, 1):
-            target[g, :, pl.ds(target.shape[2] - LANES, LANES)] = jnp.zeros((2, LANES), jnp.float32)
-            target[g, :, pl.ds(0, edges.shape[1])] = edges[2 * g : 2 * g + 2]
-
-    def both_kinds(a, b):
-        return jnp.where(iota(a.shape, 1) % 2 == 0, a, roll(b, 1, 1))
-
-    for load in loads[5 : 2 + TABLES]:
-        load.wait()
     tops = [jnp.where(lane2 < n, both(txr.at[g]), 0.0) for g in (0, 1)]
     beside = columns(jnp.concatenate(tops, axis=0), fine_place[...])[0:n]
     v = lift_groups(kinds(zr[0], zr[1]), beside, q)
     outer_rims = ends(v)
+    lifted[...] = v
     rim[...] = lift_rows(v, none, none)
     border = [rim[pl.ds(0, half, stride=2), :]]
-    even = halves(src, 0)
-    before = [p - 0.5 * e for p, e in zip(halves(xr, 0), even)]
-    stack = []
-    for k in range(px // 2):
-        after = halves(src, 2 * k + 2) if 2 * k + 2 < px else halves(xr, 1)
-        detail = [o - 0.5 * (e + a) for o, e, a in zip(halves(src, 2 * k + 1), even, after)]
-        smooth = [e + 0.25 * (b + d) for e, b, d in zip(even, before, detail)]
-        work[2 * k, 0:half], work[2 * k, half:] = smooth
-        work[2 * k + 1, 0:half], work[2 * k + 1, half:] = detail
-        stack.append((lift_halves(smooth, none, none)[0], 2 * k, 0))
-        even, before = after, detail
-        if len(stack) == BATCH:
-            for x, _, v in lift_last(stack, border):
-                ghost[pl.ds(x // 2 * half, half), :] = v
-            stack = []
-    beyond = [ends(xr[g]) for g in (0, 1)]
-    raw = []
-    for g in (0, 1):
-        yl[g] = lift_rows(ys[g], beyond[0][g], beyond[1][g])
-        raw.append(yl[g, pl.ds(0, ax, stride=2), :])
-    raw = mix_lanes(jnp.concatenate(raw, axis=0), fine_lanes[...])
-    turned = []
-    for v in outer_rims:
-        v = jnp.broadcast_to(v, (8, LANES))
-        for start in range(0, ax, 8):
-            tile = jnp.zeros((8, LANES), jnp.float32)
-            for i in range(8):
-                tile = jnp.where(row8 == i, roll(v, LANES - 2 - 2 * q * (start + i), 1), tile)
-            turned.append(tile)
-    raw = raw + jnp.concatenate(turned, axis=0) * share[0:1]
-    grown[pl.ds(own + pair + 16, py_rows), :] = raw
-    grown[pl.ds(own + pair + 24 + py_rows, 8), :] = jnp.zeros((8, LANES), jnp.float32)
-
-    halo = mix_rows(send_y[...], ghost[...])
+    near_x = mix_lanes(jnp.concatenate((xr[0, 0:half], xr[1, 0:half]), axis=0), fine_lanes[...])
+    terms = {0: 0.25 * near_x[0:half], px - 2: -0.125 * near_x[half:]}
+    for x in range(0, px, 2):
+        spot = (pl.ds(x // 2 * half, half), slice(None))
+        v = roll(border[0], LANES - 2 - q * x, 1) * share
+        grown[spot] = grown[spot] + (v + terms[x] if x in terms else v)
+    halo = mix_rows(send_y[...], grown[0:own])
     halo = (halo[0:py_rows], halo[py_rows : 2 * py_rows], halo[2 * py_rows :])
     sent[px_rows:pair] = both_kinds(halo[0], halo[1])
     sent[pair : pair + 16] = halo[2]
@@ -502,40 +498,61 @@
     for gy in (0, 1):
         rows_copy(px_rows + ax * gy, ax, (0, step_to[gy], 0))
     sent_rows = launch(copies, m_send, m_recv)
+    def along_x(rims):
+        rows = jnp.concatenate([yl[g, pl.ds(0, ax, stride=2), :] for g in (0, 1)], axis=0)
+        turned = []
+        for v in rims:
+            v = jnp.broadcast_to(v, (8, LANES))
+            for start in range(0, ax, 8):
+                tile = jnp.zeros((8, LANES), jnp.float32)
+                for i in range(8):
+                    tile = jnp.where(row8 == i, roll(v, LANES - 2 - 2 * q * (start + i), 1), tile)
+                turned.append(tile)
+        return mix_lanes(rows, fine_lanes[...]) + jnp.concatenate(turned, axis=0) * share[0:1]
+
+    beyond = [(xe[2 * g], xe[2 * g + 1]) for g in (0, 1)]
+    for g in (0, 1):
+        yl[g] = lift_rows(ys[g], beyond[0][g], beyond[1][g])
+    raw = along_x(outer_rims)
+    grown[pl.ds(own + pair + 16, py_rows), :] = raw
+    grown[pl.ds(own + pair + 24 + py_rows, 8), :] = jnp.zeros((8, LANES), jnp.float32)
     settle(grown.at[pl.ds(0, y_rows)], y_send, y_recv)
 
     tops = []
     for g in (0, 1):
         yl[g] = lift_rows(yr[g], er[g], er[2 + g])
         v = jnp.where(lane2 == n, both(tcr.at[g, 0]), both(tcr.at[g, 1]))
-        v = jnp.where(lane2 < n, both(txr.at[g]), v)
-        tops.append(jnp.where(lane2 < n + 2, v, 0.0))
-    beside = columns(jnp.concatenate(tops, axis=0), fine_place[...])[0 : n + 8]
-    lower = under((kinds(dr[0], dr[2]), kinds(dr[1], dr[3])))
-    v = lift_groups(jnp.concatenate((kinds(zr[0], zr[1]), lower), axis=0), beside, q)
-    v = lift_rows(v[0:n], v[n : n + 1], v[n + 1 : n + 2])
-    rim[...] = v
-    border = [rim[pl.ds(start, half, stride=2), :] for start in (0, 1)]
-    stack = []
-    for x in range(0, px, 2):
-        smooth = lift_halves(stored(x), yl[0, x : x + 1, :], yl[1, x : x + 1, :])
-        work[x, half:] = smooth[1]
-        stack.append((smooth[0], x, 0))
-        if len(stack) == BATCH:
-            for at, _, v in lift_last(stack, border):
-                work[at, 0:half] = v
-                grown[pl.ds(at // 2 * half, half), :] = v
-            stack = []
+        tops.append(jnp.where(lane2 // 2 == n // 2, v, 0.0))
+    beside = columns(jnp.concatenate(tops, axis=0), fine_place[...])[n : n + 8]
+    lower = lift_groups(under((kinds(dr[0], dr[2]), kinds(dr[1], dr[3]))), beside, q)
+    lower = (lower[0:1], lower[1:2])
+    late = along_x(lower)
+    for at, scale, v in ((0, 0.25, late[0:ax]), (ay - 1, -0.125, late[ax:])):
+        spot = (pl.ds(at, ax, stride=ay), slice(None))
+        grown[spot] = grown[spot] + scale * v
 
     def finish():
         energy = kept = jnp.zeros((half, LANES), jnp.float32)
+        rim[...] = lift_rows(lifted[...], *lower)
+        border = [rim[pl.ds(start, half, stride=2), :] for start in (0, 1)]
+
+        def fixed(x):
+            smooth, detail = stored(x)
+            for plane, kind, scale in ((0, 0, 0.25), (px - 2, 1, -0.125), (px - 1, 1, -0.5)):
+                if x == plane:
+                    smooth = smooth + scale * xr[kind, 0:half]
+                    detail = detail + scale * xr[kind, half:]
+            below, above = yl[0, x : x + 1, :], yl[1, x : x + 1, :]
+            smooth = smooth + jnp.where(row == 0, 0.25 * below, jnp.where(row == half - 1, -0.125 * above, 0.0))
+            return smooth, detail + jnp.where(row == half - 1, -0.5 * above, 0.0)
+
         for start in range(0, px, 4):
             stack, ready = [], []
             for x in range(start, start + 4, 2):
-                ready.append((x, 0, work[x, 0:half]))
-                stack.append((work[x, half:], x, 1))
-                lifted = lift_halves(stored(x + 1), yl[0, x + 1 : x + 2, :], yl[1, x + 1 : x + 2, :])
-                stack += [(lifted[0], x + 1, 0), (lifted[1], x + 1, 1)]
+                ready.append((x, 0, grown[pl.ds(x // 2 * half, half), :]))
+                stack.append((fixed(x)[1], x, 1))
+                whole = fixed(x + 1)
+                stack += [(whole[0], x + 1, 0), (whole[1], x + 1, 1)]
             for x, kind, v in (*ready, *lift_last(stack, border)):
                 small = shrink(v, level_thresh)
                 out[0, x, pl.ds(kind, half, stride=2), :] = small
@@ -576,7 +593,7 @@
     cut = LANES - reach * (deep - 1)
     rest = reach - cut
 
-    def spread(source, target, send_sem, recv_sem):
+    def spread(source, target, send_sem, recv_sem, first=0, last=None):
         def post(j):
             return pltpu.make_async_remote_copy(
                 src_ref=source, dst_ref=target, send_sem=send_sem, recv_sem=recv_sem,
@@ -588,9 +605,10 @@
             return carry
 
         if ndev <= 32:
-            for j in sorted(range(1, ndev), key=lambda j: (-distance(split(j)), j)):
+            order = sorted(range(1, ndev), key=lambda j: (-distance(split(j)), j))
+            for j in order[first:last]:
                 post(j).start()
-        else:
+        elif first == 0:
             lax.fori_loop(1, ndev, send, 0)
 
     pieces = mix_rows(reach_rows[...], here)
@@ -610,7 +628,7 @@
     for x in range(1, long):
         spare += roll(loose[x : x + 1], rest * x, 1)
     msg[...] = jnp.where(row8 == long, spare, sheet)
-    spread(msg, gath.at[slot], g_send, g_recv)
+    spread(msg, gath.at[slot], g_send, g_recv, 0, ndev // 2)
     gath[slot] = msg[...]
     sums = finish()
     quarter = own // 4
@@ -623,6 +641,7 @@
 
     o1s[...], early = level_rows(mix_lanes(here, lanes12[...]), pl.ds(0, own))
     o2s[...] = early.reshape(o2s.shape)
+    spread(msg, gath.at[slot], g_send, g_recv, ndev // 2)
     settle(grown.at[pl.ds(0, sent_rows)], m_send, m_recv)
 
     for g in (0, 1):
@@ -695,14 +714,17 @@
                 v += sum(window(spares[z], rest * x, cz * z + cut, rest) for z in range(nz))
             parts_s[pl.ds((y * long + x) * spots, spots), :] = v
 
-    def dot(a, b):
-        return jnp.dot(a, b, precision=lax.Precision.HIGHEST, preferred_element_type=jnp.float32)
-
+    filled = long * deep * spots
+    spare_rows = parts_s.shape[0] - filled
+    if spare_rows:
+        parts_s[pl.ds(filled, spare_rows), :] = jnp.zeros((spare_rows, LANES), jnp.float32)
     grid = parts_s[...]
     loads[2 + TABLES].wait()
     loads[3 + TABLES].wait()
-    half3, half4 = dot(k_s[0], grid), dot(k_s[1], grid)
-    grid, grid4 = dot(half3, l_s[0]), dot(half4, l_s[1])
+    cells_in = spots * count
+    grid = mix_rows(k_s[...], grid)
+    half3, half4 = grid[0:cells_in], doubled(grid[cells_in:], cells_in)
+    grid, grid4 = mix_lanes(half3, l_s[0]), mix_lanes(half4, l_s[1])
     row = iota(grid.shape, 0)
     lane = iota(grid.shape, 1)
     inner_row = row % count
@@ -768,14 +790,15 @@
     middle = fine_tables(lx) + reach_tables(lx // 2, ly // 2, lz // 2) + middle
     scratch = [
         *(pltpu.VMEM(shape, jnp.float32) for shape in (
-            (2, ly, LANES), (2, ly, LANES), (2, lx, LANES), (2, lx, LANES), (4, 1, LANES), (4, 1, LANES),
+            (2, ly, LANES), (2, ly, LANES), (4, 1, LANES), (2, ly, LANES), (2, lx, LANES), (2, lx, LANES),
+            (4, 1, LANES), (4, 1, LANES),
             (2, lx, LANES), (ly, LANES), (2, ly, LANES), (2, 1, LANES), (4, 1, LANES), (2, 2, LANES),
             (2, 2, 2, LANES), (2, 2, 2, 2, LANES), (ly, LANES), (lx, ly, LANES),
         )),
         pltpu.SemaphoreType.DMA,
         pltpu.SemaphoreType.DMA,
         *(pltpu.VMEM(shape, jnp.float32) for shape in (
-            (own + 2 * lx + ly + 32, LANES), (own, LANES), (lx + ly + 24, LANES), (2, 2, 2 * LANES),
+            (own + 2 * lx + ly + 32, LANES), (ly, LANES), (lx + ly + 24, LANES), (2, 2, 2 * LANES),
             (2, 2, own + 2 * LANES), (2, 2, own + 2 * LANES), (2, 2, 2, 2 * LANES), (2, 2, 2, LANES),
             (2, 2, 2, 2, LANES), (own, LANES), (lx // 4, ly // 4, LANES),
         )),
@@ -787,15 +810,15 @@
     scratch += [
         pltpu.VMEM((ndev, 8, LANES), jnp.float32),
         pltpu.VMEM((8, LANES), jnp.float32),
-        pltpu.VMEM((tables[0].shape[2], LANES), jnp.float32),
+        pltpu.VMEM((tables[0].shape[1], LANES), jnp.float32),
         pltpu.VMEM((nx * ny * count, LANES), jnp.float32),
         pltpu.VMEM((1, LANES), jnp.float32),
         pltpu.VMEM((ndev, 1, LANES), jnp.float32),
         *[pltpu.SemaphoreType.DMA] * 4,
         pltpu.VMEM(fields.shape, jnp.float32),
         pltpu.SMEM(exponents.shape, jnp.int32),
-        pltpu.VMEM(tables[0].shape, jnp.float32),
-        pltpu.VMEM(tables[1].shape, jnp.float32),
+        pltpu.VMEM(tables[0].shape, jnp.bfloat16),
+        pltpu.VMEM(tables[1].shape, jnp.bfloat16),
         pltpu.SemaphoreType.DMA((4 + TABLES,)),
         *(pltpu.VMEM(table.shape, table.dtype) for table in middle),
     ]

time: 21.8 us -> 21.7 us (level)
  no operation moved by 1% of the time
where the time goes in v8:
time: 21.7 us; the launch traced here: 21.6 us
  Pallas kernels  20.9 us (96%)
  between operations  0.64 us (3%)
    pallas_call x1, Pallas kernels, shards(): pl.pallas_call(functools.partial(kernel, sizes, cells), out_shape=(pltpu....  20.1 us
    pallas_call x1, Pallas kernels, shards(): pl.pallas_call(deliver, out_shape=(jax.ShapeDtypeStruct(fields.shape, jnp...  0.83 us

profile of v8, /device:TPU:0, one launch (start us, length us, event | category | flops | bytes accessed | tf_op | source)
XLA Modules:
  0.0 21.6 jit_solution(11379754588770352383)
XLA Ops:
  0.6 20.1 %shard_map.185 = (f32[1,32,32,128]{3,2,1,0:T(8,128)S(1)}, f32[2,1,5]{2,1,0:T(1,128)S(1)}) custom-call(s32[5]{0:T(128)} %exps_in.1, f32[1,32,32,128]{3,2,1,0:T(8,128)} %field_in.1, bf16[384,400]{1,0:T(8,128)(2,1)} %constant.32.clone.rows_in, bf16[2,128,128]{2,1,0:T(8,128)(2,1)} %constant.33.clone.lanes_in, bf16[128,128]{1,0:T(8,128)(2,1)} %constant.34.clone.rest_0_, ...), custom_call_target="tpu_custom_call" | custom-call | tf_op jit(solution)/shard_map/pallas_call | solution.py:826
  20.7 0.8 %shard_map.186 = (f32[1,32,32,128]{3,2,1,0:T(8,128)}, f32[2,1,5]{2,1,0:T(1,128)}) custom-call(f32[1,32,32,128]{3,2,1,0:T(8,128)S(1)} %get-tuple-element.4.held, f32[2,1,5]{2,1,0:T(1,128)S(1)} %get-tuple-element.5.held_stats), custom_call_target="tpu_custom_call" | custom-call | tf_op jit(solution)/shard_map/pallas_call | solution.py:840

commit v9 on v8

--- a/solution.py
+++ b/solution.py
@@ -14,7 +14,6 @@
 LANES = 128
 CHUNKS = 4
 BUFFERS = 20
-TABLES = 14
 BATCH = 8
 ROUNDS = 2
 VMEM_LIMIT = 58_720_256
@@ -263,16 +262,18 @@
     return jnp.sum(jnp.sum(v, axis=0, keepdims=True), axis=1, keepdims=True)
 
 
-def kernel(sizes, cells, exps_in, field_in, rows_in, lanes_in, *rest):
-    tables_in, (out, stats), scratch = rest[:TABLES], rest[TABLES : TABLES + 2], rest[TABLES + 2 :]
+def kernel(sizes, cells, layout, exps_in, field_in, rows_in, lanes_in, *rest):
+    packs = 1 + max(pack for pack, _, _ in layout)
+    tables_in, (out, stats), scratch = rest[:packs], rest[packs : packs + 2], rest[packs + 2 :]
     nx, ny, nz = sizes
     ndev = nx * ny * nz
     scratch = list(scratch)
-    tables = scratch[-TABLES:]
-    scratch = scratch[:-TABLES]
+    held = scratch[-packs:]
+    scratch = scratch[:-packs]
+    tables = [held[pack].at[pl.ds(start, size)] for pack, start, size in layout]
     field, exps, k_s, l_s, in_sem = scratch[-5:]
     scratch = scratch[:-5]
-    pairs = [(field_in, field), (exps_in, exps), *zip(tables_in, tables), (rows_in, k_s), (lanes_in, l_s)]
+    pairs = [(field_in, field), (exps_in, exps), *zip(tables_in, held), (rows_in, k_s), (lanes_in, l_s)]
     loads = [pltpu.make_async_copy(a, b, in_sem.at[i]) for i, (a, b) in enumerate(pairs)]
     me = (lax.axis_index("gx"), lax.axis_index("gy"), lax.axis_index("gz"))
 
@@ -395,7 +396,7 @@
     packed = jnp.where(lane % q == 2, odd_end, even_end)
     zs[...] = packed
     ds[0], ds[1] = ends(packed)
-    for load in loads[2:5]:
+    for load in loads[2 : 2 + packs]:
         load.wait()
     edges = sum(
         mix(fine_edges[...], part, ((1,), (1,)))
@@ -432,8 +433,6 @@
     sent_rows = launch(others, send_sem, recv_sem)
     y_rows += launch(along_y[-2:], y_send, y_recv)
 
-    for load in loads[5 : 2 + TABLES]:
-        load.wait()
     even = halves(src, 0)
     before = [-0.5 * e for e in even]
     stack = []
@@ -719,8 +718,8 @@
     if spare_rows:
         parts_s[pl.ds(filled, spare_rows), :] = jnp.zeros((spare_rows, LANES), jnp.float32)
     grid = parts_s[...]
-    loads[2 + TABLES].wait()
-    loads[3 + TABLES].wait()
+    loads[2 + packs].wait()
+    loads[3 + packs].wait()
     cells_in = spots * count
     grid = mix_rows(k_s[...], grid)
     half3, half4 = grid[0:cells_in], doubled(grid[cells_in:], cells_in)
@@ -776,6 +775,16 @@
         copy.wait()
 
 
+def pack_tables(tables):
+    groups, layout = {}, []
+    for table in tables:
+        group = groups.setdefault(table.shape[1], [])
+        start = sum(len(part) for part in group)
+        layout.append((list(groups).index(table.shape[1]), start, len(table)))
+        group.append(np.pad(table, ((0, -len(table) % 16), (0, 0))))
+    return [np.concatenate(group) for group in groups.values()], layout
+
+
 def shards(sizes, fields, exponents):
     nx, ny, nz = sizes
     ndev = nx * ny * nz
@@ -787,7 +796,7 @@
     tables = coarse_matrices(sizes, coarse)
     middle = middle_tables(lx // 2, ly // 2, lz // 2)
     own, extra = lx // 2 * (ly // 2), middle[0].shape[0]
-    middle = fine_tables(lx) + reach_tables(lx // 2, ly // 2, lz // 2) + middle
+    middle, layout = pack_tables(fine_tables(lx) + reach_tables(lx // 2, ly // 2, lz // 2) + middle)
     scratch = [
         *(pltpu.VMEM(shape, jnp.float32) for shape in (
             (2, ly, LANES), (2, ly, LANES), (4, 1, LANES), (2, ly, LANES), (2, lx, LANES), (2, lx, LANES),
@@ -819,17 +828,17 @@
         pltpu.SMEM(exponents.shape, jnp.int32),
         pltpu.VMEM(tables[0].shape, jnp.bfloat16),
         pltpu.VMEM(tables[1].shape, jnp.bfloat16),
-        pltpu.SemaphoreType.DMA((4 + TABLES,)),
+        pltpu.SemaphoreType.DMA((4 + len(middle),)),
         *(pltpu.VMEM(table.shape, table.dtype) for table in middle),
     ]
     vmem = pl.BlockSpec(memory_space=pltpu.VMEM)
     held = pl.pallas_call(
-        functools.partial(kernel, sizes, cells),
+        functools.partial(kernel, sizes, cells, layout),
         out_shape=(
             pltpu.VMEM(fields.shape, jnp.float32),
             pltpu.VMEM((2, 1, LEVELS), jnp.float32),
         ),
-        in_specs=[pl.BlockSpec(memory_space=pltpu.HBM)] * (4 + TABLES),
+        in_specs=[pl.BlockSpec(memory_space=pltpu.HBM)] * (4 + len(middle)),
         out_specs=(vmem, vmem),
         scratch_shapes=scratch,
         compiler_params=pltpu.CompilerParams(

time: 21.7 us -> 21.6 us (level)
  no operation moved by 1% of the time
where the time goes in v9:
time: 21.6 us; the launch traced here: 21.5 us
  Pallas kernels  20.8 us (96%)
  between operations  0.64 us (3%)
    pallas_call x1, Pallas kernels, shards(): pl.pallas_call(functools.partial(kernel, sizes, cells, layout), out_shape...  20 us
    pallas_call x1, Pallas kernels, shards(): pl.pallas_call(deliver, out_shape=(jax.ShapeDtypeStruct(fields.shape, jnp...  0.83 us

profile of v9, /device:TPU:0, one launch (start us, length us, event | category | flops | bytes accessed | tf_op | source)
XLA Modules:
  0.0 21.5 jit_solution(14610655596981856125)
XLA Ops:
  0.6 20.0 %shard_map.95 = (f32[1,32,32,128]{3,2,1,0:T(8,128)S(1)}, f32[2,1,5]{2,1,0:T(1,128)S(1)}) custom-call(s32[5]{0:T(128)} %exps_in.1, f32[1,32,32,128]{3,2,1,0:T(8,128)} %field_in.1, bf16[384,400]{1,0:T(8,128)(2,1)} %constant.12.clone.rows_in, bf16[2,128,128]{2,1,0:T(8,128)(2,1)} %constant.13.clone.lanes_in, bf16[1200,128]{1,0:T(8,128)(2,1)} %constant.14.clone.rest_0_, ...), custom_call_target="tpu_custom_call" | custom-call | tf_op jit(solution)/shard_map/pallas_call | solution.py:835
  20.6 0.8 %shard_map.96 = (f32[1,32,32,128]{3,2,1,0:T(8,128)}, f32[2,1,5]{2,1,0:T(1,128)}) custom-call(f32[1,32,32,128]{3,2,1,0:T(8,128)S(1)} %get-tuple-element.4.held, f32[2,1,5]{2,1,0:T(1,128)S(1)} %get-tuple-element.5.held_stats), custom_call_target="tpu_custom_call" | custom-call | tf_op jit(solution)/shard_map/pallas_call | solution.py:849
